TPU v7x, 256 devices: a whole 4x4x8 slice. The times are simulated.
256 devices in a mesh: section: 2 (over x_lo), slab: 128 (over y, x_hi, z, core).
Axes of the slice: x: 4 (x_hi: 2, x_lo: 2; x = x_hi * 2 + x_lo), y: 4, z: 8, core: 2. Of those that a mesh axis runs over, the one named last changes fastest.
Arguments:
- concentration: float32 [4, 2048, 2048], P('section', 'slab'), may hold values from -3.2 to 3.2
Outputs:
- new_concentration: float32 [4, 2048, 2048], P('section', 'slab')
- energy: float32 [], replicated
All inputs are finite; a program needn't handle non-finite values.
Results may differ from a plain program's by a relative error of at most 0.000098.
Values sent between devices are 32-bit elements; how exact they have to be, the bound alone decides.
No kernel may reach another device: no remote copies, remote signals or barrier semaphores. Data moves between devices by JAX's collectives and lax.ppermute only.
A program may use at most 64 MiB of HBM per device.

v0:
```python
import math

import jax
import jax.numpy as jnp
import ml_dtypes
import numpy as np
from jax import lax
from jax.experimental import pallas as pl
from jax.experimental.pallas import tpu as pltpu
from jax.sharding import PartitionSpec as P

ALL = ("section", "slab")
NX = 2048
NY = 2048
NZ = 4
CELLS = NX * NY * NZ
time_step = 100.0
kappa_grad = 2.0
stabilizer = 8.0
f32 = jnp.float32
bf16 = jnp.bfloat16


def halves(matrix):
    high = matrix.astype(np.float32).astype(ml_dtypes.bfloat16)
    low = (matrix - high.astype(np.float64)).astype(np.float32).astype(ml_dtypes.bfloat16)
    return np.stack([high, low])


def fourier_table():
    index = np.arange(128)
    angle = 2.0 * np.pi * (np.outer(index, index) % 128) / 128
    return halves(np.block([[np.cos(angle), np.sin(angle)], [-np.sin(angle), np.cos(angle)]]))


def real_table():
    angle = 2.0 * np.pi * (np.outer(np.arange(128), np.arange(256)) % 256) / 256
    lower = -np.sin(angle)
    lower[0] = 1.0 - 2.0 * (np.arange(256) % 2)
    return halves(np.concatenate([np.cos(angle), lower], 0))


def lane_table(parity):
    z_at, x_at = np.arange(2)[:, None, None, None], np.arange(16)[None, :, None, None]
    t_at, q_at = np.arange(2)[None, None, :, None], np.arange(16)[None, None, None, :]
    turn = (4 * parity * z_at + 8 * t_at * z_at + x_at * q_at) % 16
    value = np.exp(-2j * np.pi * turn / 16).reshape(32, 32)
    value = np.kron(np.eye(4), value)
    return halves(np.block([[value.real, value.imag], [-value.imag, value.real]]))


def y_twist_table():
    angle = 2.0 * np.pi * np.outer(np.arange(8), np.arange(128)) / 2048
    return np.concatenate([np.cos(angle), np.sin(angle)], 0).astype(np.float32)


def x_twist_table():
    angle = 2.0 * np.pi * np.outer(np.arange(128), np.arange(128) % 16) / 2048
    return np.stack([np.cos(angle), np.sin(angle)]).astype(np.float32)


FOURIER = fourier_table()
REAL = real_table()
LANES = np.stack([lane_table(0), lane_table(1)])
Y_TWIST = y_twist_table()
X_TWIST = x_twist_table()
COS16 = [math.cos(2.0 * math.pi * m / 16) for m in range(16)]
SIN16 = [math.sin(2.0 * math.pi * m / 16) for m in range(16)]


def split(value):
    high = value.astype(bf16)
    return high, (value - high.astype(f32)).astype(bf16)


NN = (((1,), (0,)), ((), ()))
NT = (((1,), (1,)), ((), ()))


def product(left, right, pattern):
    def one(a, b):
        return lax.dot_general(a, b, pattern, preferred_element_type=f32)

    return one(left[0], right[0]) + (one(left[1], right[0]) + one(left[0], right[1]))


def weighted(terms):
    total = None
    for weight, value in terms:
        if abs(weight) < 1e-12:
            continue
        if abs(weight - 1.0) < 1e-12:
            part = value
        elif abs(weight + 1.0) < 1e-12:
            part = -value
        else:
            part = value * weight
        total = part if total is None else total + part
    return total


def y_slots(field, twist):
    at = [field[:, 128 * a : 128 * a + 128] for a in range(16)]
    add = [at[a] + at[a + 8] for a in range(8)]
    sub = [at[a] - at[a + 8] for a in range(8)]
    slots = [
        jnp.concatenate([(add[0] + add[4]) + (add[2] + add[6]), (add[1] + add[5]) + (add[3] + add[7])], 1)
    ]
    real, imag = {}, {}
    for j in (2, 4, 6):
        real[j] = weighted([(COS16[j * a % 16], add[a]) for a in range(8)])
        imag[j] = weighted([(-SIN16[j * a % 16], add[a]) for a in range(8)])
    minus = [None] + [sub[a] - sub[8 - a] for a in (1, 2, 3)]
    plus = [None] + [sub[a] + sub[8 - a] for a in (1, 2, 3)] + [sub[4]]
    for j in (1, 3, 5, 7):
        real[j] = weighted([(1.0, sub[0])] + [(COS16[j * a % 16], minus[a]) for a in (1, 2, 3)])
        imag[j] = weighted([(-SIN16[j * a % 16], plus[a]) for a in (1, 2, 3, 4)])
    for j in range(1, 8):
        cos, sin = twist[j : j + 1], twist[8 + j : 9 + j]
        slots.append(
            jnp.concatenate([real[j] * cos + imag[j] * sin, imag[j] * cos - real[j] * sin], 1)
        )
    return slots


def forward_y(field, fourier, real_rows, twist, put):
    squared = field * field
    bulk = squared * (0.25 * squared - 0.5)
    cubic = squared * field - field
    for f, value in ((0, field), (1, cubic)):
        slots = y_slots(value, twist)
        first = product(real_rows, split(slots[0]), NT)
        for h in (0, 1):
            rows = jnp.concatenate(slots[4 * h : 4 * h + 4], 0)
            out = product(fourier, split(rows), NT)
            if h == 0:
                lane = lax.broadcasted_iota(jnp.int32, (256, 128), 1)
                wide = jnp.concatenate([first] * 4, 1)
                out = jnp.where(lane < 32, wide, out)
            put(h, 0, f, out[:128])
            put(h, 1, f, out[128:])
    lanes = sum(bulk[:, 128 * a : 128 * a + 128] for a in range(16))
    return lanes


def wave_square(index, length):
    signed = jnp.where(2 * index >= length, index - length, index)
    phase_angle = signed.astype(f32) * (2.0 * math.pi / length)
    return phase_angle * phase_angle


def rates(wave_sq):
    numerator = 1.0 + time_step * stabilizer * wave_sq
    inverse = 1.0 / (numerator + time_step * kappa_grad * wave_sq * wave_sq)
    return numerator * inverse, time_step * wave_sq * inverse


def middle(get, section_at, slab_at, fourier, lanes, twist, put):
    lane = lax.broadcasted_iota(jnp.int32, (128, 128), 1)
    row = lax.broadcasted_iota(jnp.int32, (128, 128), 0)
    packed = (lane < 32) & (section_at == 0) & (slab_at == 0)
    cos, sin = twist[0], twist[1]
    parts = []
    for s in (0, 1):
        c_re, c_im, g_re, g_im = get(s, 0, 0), get(s, 1, 0), get(s, 0, 1), get(s, 1, 1)
        c_im, g_re = jnp.where(packed, g_re, c_im), jnp.where(packed, c_im, g_re)
        parts.append((c_re, c_im, g_re, g_im))
    stacked = []
    for sigma in (0, 1):
        mixed = [a + b if sigma == 0 else a - b for a, b in zip(*parts)]
        stacked.append(
            jnp.concatenate(
                [jnp.concatenate([mixed[0], mixed[2]], 1), jnp.concatenate([mixed[1], mixed[3]], 1)], 0
            )
        )
    slot = 4 * section_at + lane // 32
    y_index = jnp.where(slot == 0, 8 * slab_at, slot + 16 * slab_at)
    x_index = row + 128 * (lane % 16)
    wave_x = wave_square(x_index, NX)
    wave_xy = wave_x + wave_square(y_index, NY)
    half_y = (2.0 * math.pi / NY * (NY // 2)) ** 2
    back = []
    for sigma in (0, 1):
        spread = product(fourier, split(stacked[sigma]), NN)
        rows = []
        for f in (0, 1):
            re, im = spread[:128, 128 * f : 128 * f + 128], spread[128:, 128 * f : 128 * f + 128]
            rows.append(jnp.concatenate([re * cos + im * sin, im * cos - re * sin], 1))
        table = (lanes[sigma, 0], lanes[sigma, 1])
        spec = product(split(jnp.concatenate(rows, 0)), table, NN)
        c_re, c_im, g_re, g_im = spec[:128, :128], spec[:128, 128:], spec[128:, :128], spec[128:, 128:]
        wave_z = wave_square(sigma + 2 * (lane // 16 % 2), NZ)
        keep, mix = rates(wave_z + wave_xy)
        keep_half, mix_half = rates(wave_z + (wave_x + half_y))
        main_re = keep * c_re - mix * jnp.where(packed, c_im, g_re)
        main_im = keep * c_im - mix * jnp.where(packed, -c_re, g_im)
        side_re = keep_half * g_re - mix_half * g_im
        side_im = keep_half * g_im + mix_half * g_re
        rows = jnp.concatenate(
            [jnp.concatenate([main_re, main_im], 1), jnp.concatenate([side_re, side_im], 1)], 0
        )
        back.append(product(split(rows), table, NT))
    for s in (0, 1):
        mixed = back[0] + back[1] if s == 0 else back[0] - back[1]
        both = []
        for f in (0, 1):
            re, im = mixed[128 * f : 128 * f + 128, :128], mixed[128 * f : 128 * f + 128, 128:]
            both.append((re * cos - im * sin, im * cos + re * sin))
        (m_re, m_im), (s_re, s_im) = both
        upper = jnp.concatenate([m_re, jnp.where(packed, s_re, m_im)], 1)
        lower = jnp.concatenate([-m_im, jnp.where(packed, -s_im, m_re)], 1)
        out = product(
            (fourier[0][:128], fourier[1][:128]), split(jnp.concatenate([upper, lower], 0)), NN
        )
        put(s, 0, out[:, :128])
        put(s, 1, out[:, 128:])


def inverse_y(get, fourier, real_rows, twist, put):
    slots = []
    for h in (0, 1):
        re, im = get(h, 0), get(h, 1)
        if h == 0:
            row = lax.broadcasted_iota(jnp.int32, (128, 128), 0)
            lane = lax.broadcasted_iota(jnp.int32, (128, 128), 1)
            single = (row == 0) & (lane < 32)
            re, im = jnp.where(single, 0.5 * re, re), jnp.where(single, 0.5 * im, im)
        rows = split(jnp.concatenate([re.T, im.T], 1))
        if h == 0:
            first = product((rows[0][:32], rows[1][:32]), real_rows, NN)
            rows = (rows[0][32:], rows[1][32:])
        out = product(rows, fourier, NN)
        slots += [out[32 * m : 32 * m + 32] for m in range(out.shape[0] // 32)]
    scale = 2.0 / CELLS
    base = [first[:, :128] * scale, first[:, 128:] * scale]
    real, imag = {}, {}
    for j in range(1, 8):
        re, im = slots[j - 1][:, :128], slots[j - 1][:, 128:]
        cos, sin = twist[j : j + 1] * scale, twist[8 + j : 9 + j] * scale
        real[j], imag[j] = re * cos - im * sin, im * cos + re * sin
    even = [
        weighted(
            [(COS16[j * a % 16], real[j]) for j in (2, 4, 6)]
            + [(-SIN16[j * a % 16], imag[j]) for j in (2, 4, 6)]
        )
        + base[a % 2]
        for a in range(8)
    ]
    cosine = [weighted([(COS16[j * a % 16], real[j]) for j in (1, 3, 5, 7)]) for a in range(4)]
    sine = [None] + [weighted([(SIN16[j * a % 16], imag[j]) for j in (1, 3, 5, 7)]) for a in range(1, 5)]
    odd = [cosine[0]] + [cosine[a] - sine[a] for a in (1, 2, 3)] + [-sine[4]]
    odd += [-cosine[a] - sine[a] for a in (3, 2, 1)]
    for a in range(8):
        put(a, even[a] + odd[a])
        put(a + 8, even[a] - odd[a])


def forward_kernel(c_ref, fourier_ref, real_ref, twist_ref, out_ref, bulk_ref):
    def put(h, part, f, value):
        at = 2 * part + f
        out_ref[128 * h : 128 * h + 128, 128 * at : 128 * at + 128] = value

    field = jnp.concatenate([c_ref[0], c_ref[1]], 0)
    lanes = forward_y(
        field, (fourier_ref[0], fourier_ref[1]), (real_ref[0], real_ref[1]), twist_ref[...], put
    )
    bulk_ref[...] = jnp.broadcast_to(jnp.sum(lanes, 0, keepdims=True), (8, 128))


def middle_kernel(in_ref, bulk_ref, fourier_ref, lanes_ref, twist_ref, out_ref):
    def get(s, part, f):
        at = 2 * part + f
        return in_ref[128 * s : 128 * s + 128, 128 * at : 128 * at + 128]

    def put(s, part, value):
        out_ref[128 * s : 128 * s + 128, 128 * part : 128 * part + 128] = value

    middle(
        get,
        lax.axis_index("section"),
        lax.axis_index("slab"),
        (fourier_ref[0], fourier_ref[1]),
        lanes_ref,
        twist_ref,
        put,
    )
    out_ref[:, 256:384] = jnp.broadcast_to(bulk_ref[0:1, :], (256, 128))


def inverse_kernel(in_ref, fourier_ref, real_ref, twist_ref, out_ref, energy_ref):
    def get(h, part):
        return in_ref[128 * h : 128 * h + 128, 128 * part : 128 * part + 128]

    def put(a, value):
        out_ref[0, :, 128 * a : 128 * a + 128] = value[:16]
        out_ref[1, :, 128 * a : 128 * a + 128] = value[16:]

    inverse_y(
        get, (fourier_ref[0], fourier_ref[1]), (real_ref[0], real_ref[1]), twist_ref[...], put
    )
    energy_ref[...] = jnp.sum(in_ref[:, 256:384], keepdims=True) * (1.0 / CELLS)


def per_device(concentration):
    whole = pl.BlockSpec(memory_space=pltpu.VMEM)
    outgoing, bulk = pl.pallas_call(
        forward_kernel,
        out_shape=(jax.ShapeDtypeStruct((256, 512), f32), jax.ShapeDtypeStruct((8, 128), f32)),
        in_specs=[whole] * 4,
        out_specs=(whole, whole),
    )(concentration, FOURIER, REAL, Y_TWIST)
    columns = lax.all_to_all(outgoing, ALL, split_axis=0, concat_axis=0, tiled=True)
    leaving = pl.pallas_call(
        middle_kernel,
        out_shape=jax.ShapeDtypeStruct((256, 384), f32),
        in_specs=[whole] * 5,
        out_specs=whole,
    )(columns, bulk, FOURIER, LANES, X_TWIST)
    rows_back = lax.all_to_all(leaving, ALL, split_axis=0, concat_axis=0, tiled=True)
    new_field, energy = pl.pallas_call(
        inverse_kernel,
        out_shape=(jax.ShapeDtypeStruct(concentration.shape, f32), jax.ShapeDtypeStruct((1, 1), f32)),
        in_specs=[whole] * 4,
        out_specs=(whole, whole),
    )(rows_back, FOURIER, REAL, Y_TWIST)
    return new_field, energy.reshape(())


def solution(mesh):
    return jax.shard_map(
        per_device,
        mesh=mesh,
        in_specs=(P("section", "slab", None),),
        out_specs=(P("section", "slab", None), P()),
        check_vma=False,
    )
```

profile of v0, /device:TPU:1, one launch (start us, length us, event | category | flops | bytes accessed | tf_op | source)
XLA Modules:
  0.0 74.3 jit_solution(18159095769490988418)
XLA Ops:
  0.6 2.7 %shard_map.77 = (f32[256,512]{1,0:T(8,128)}, f32[8,128]{1,0:T(8,128)}) custom-call(f32[2,16,2048]{2,1,0:T(8,128)} %c_ref.1, bf16[2,256,256]{2,1,0:T(8,128)(2,1)} %constant.10.clone.fourier_ref, bf16[2,256,256]{2,1,0:T(8,128)(2,1)} %constant.11.clone.real_ref, f32[16,128]{1,0:T(8,128)} %constant.12.clone.twist_ref), custom_call_target="tpu_custom_call" | custom-call | tf_op jit(solution)/shard_map/pallas_call | solution.py:306
  3.3 1.6 %copy.8 = f32[256,1,512]{2,1,0:T(1,128)S(1)} copy(f32[256,1,512]{2,0,1:T(8,128)} %bitcast.12) | data formatting | bytes 1048576 | tf_op jit(solution)/shard_map/all_to_all | solution.py:312
  4.9 35.8 %all_to_all.22 = f32[256,1,512]{2,1,0:T(1,128)S(1)} all-to-all(f32[256,1,512]{2,1,0:T(1,128)S(1)} %copy.8), channel_id=1, replica_groups=mesh['section'=2,'slab'=128] {'section','slab'}, dimensions={0} | all-to-all | bytes 1048576 | tf_op jit(solution)/shard_map/all_to_all | solution.py:312
  40.8 0.8 %copy.14 = f32[256,1,512]{2,0,1:T(8,128)} copy(f32[256,1,512]{2,1,0:T(1,128)S(1)} %all_to_all.22) | data formatting | bytes 1048576
  41.6 3.9 %shard_map.78 = f32[256,384]{1,0:T(8,128)} custom-call(f32[256,512]{1,0:T(8,128)} %bitcast.9, f32[8,128]{1,0:T(8,128)} %get-tuple-element.7.bulk_ref, bf16[2,256,256]{2,1,0:T(8,128)(2,1)} %constant.10.clone.fourier_ref, bf16[2,2,256,256]{3,2,1,0:T(8,128)(2,1)} %constant.13.clone.lanes_ref, f32[2,128,128]{2,1,0:T(8,128)} %constant.14.clone.twist_ref), custom_call_target="tpu_custom_call" | custom-call | tf_op jit(solution)/shard_map/pallas_call | solution.py:313
  45.5 1.4 %copy.9 = f32[256,1,384]{2,1,0:T(1,128)S(1)} copy(f32[256,1,384]{2,0,1:T(8,128)} %bitcast.11) | data formatting | bytes 786432 | tf_op jit(solution)/shard_map/all_to_all | solution.py:319
  46.9 24.4 %all_to_all.23 = f32[256,1,384]{2,1,0:T(1,128)S(1)} all-to-all(f32[256,1,384]{2,1,0:T(1,128)S(1)} %copy.9), channel_id=1, replica_groups=mesh['section'=2,'slab'=128] {'section','slab'}, dimensions={0} | all-to-all | bytes 786432 | tf_op jit(solution)/shard_map/all_to_all | solution.py:319
  71.2 0.8 %copy.15 = f32[256,1,384]{2,0,1:T(8,128)} copy(f32[256,1,384]{2,1,0:T(1,128)S(1)} %all_to_all.23) | data formatting | bytes 786432
  72.0 2.3 %shard_map.79 = (f32[2,16,2048]{2,1,0:T(8,128)}, f32[1,1]{1,0:T(1,128)}) custom-call(f32[256,384]{1,0:T(8,128)} %bitcast.10, bf16[2,256,256]{2,1,0:T(8,128)(2,1)} %constant.10.clone.fourier_ref, bf16[2,256,256]{2,1,0:T(8,128)(2,1)} %constant.11.clone.real_ref, f32[16,128]{1,0:T(8,128)} %constant.12.clone.twist_ref), custom_call_target="tpu_custom_call" | custom-call | tf_op jit(solution)/shard_map/pallas_call | solution.py:320
where the time goes:
time: 74.6 us; the launch traced here: 74.3 us
  blocking collectives  60.2 us (81%)
  Pallas kernels  8.88 us (12%)
  local copies, waits for them, and re-layouts  4.56 us (6%)
    all_to_all x1, blocking collectives, per_device(): lax.all_to_all(outgoing, ALL, split_axis=0, concat_axis=0, tiled=True)  35.8 us
    all_to_all x1, blocking collectives, per_device(): lax.all_to_all(leaving, ALL, split_axis=0, concat_axis=0, tiled=True)  24.4 us
    pallas_call x1, Pallas kernels, per_device(): pl.pallas_call(middle_kernel, out_shape=jax.ShapeDtypeStruct((256, 384),...  3.87 us
    pallas_call x1, Pallas kernels, per_device(): pl.pallas_call(forward_kernel, out_shape=(jax.ShapeDtypeStruct((256, 512)...  2.72 us
    pallas_call x1, Pallas kernels, per_device(): pl.pallas_call(inverse_kernel, out_shape=(jax.ShapeDtypeStruct(concentrat...  2.29 us
    unnamed x2, local copies, waits for them, and re-layouts  1.58 us
    all_to_all x1, local copies, waits for them, and re-layouts, per_device(): lax.all_to_all(outgoing, ALL, split_axis=0, concat_axis=0, tiled=True)  1.58 us

commit v1 on v0

--- a/solution.py
+++ b/solution.py
@@ -257,8 +257,7 @@
 
 def forward_kernel(c_ref, fourier_ref, real_ref, twist_ref, out_ref, bulk_ref):
     def put(h, part, f, value):
-        at = 2 * part + f
-        out_ref[128 * h : 128 * h + 128, 128 * at : 128 * at + 128] = value
+        out_ref[pl.ds(512 * h + 2 * part + f, 128, stride=4), :] = value
 
     field = jnp.concatenate([c_ref[0], c_ref[1]], 0)
     lanes = forward_y(
@@ -269,11 +268,10 @@
 
 def middle_kernel(in_ref, bulk_ref, fourier_ref, lanes_ref, twist_ref, out_ref):
     def get(s, part, f):
-        at = 2 * part + f
-        return in_ref[128 * s : 128 * s + 128, 128 * at : 128 * at + 128]
+        return in_ref[pl.ds(512 * s + 2 * part + f, 128, stride=4), :]
 
     def put(s, part, value):
-        out_ref[128 * s : 128 * s + 128, 128 * part : 128 * part + 128] = value
+        out_ref[pl.ds(384 * s + part, 128, stride=3), :] = value
 
     middle(
         get,
@@ -284,12 +282,12 @@
         twist_ref,
         put,
     )
-    out_ref[:, 256:384] = jnp.broadcast_to(bulk_ref[0:1, :], (256, 128))
+    out_ref[pl.ds(2, 256, stride=3), :] = jnp.broadcast_to(bulk_ref[0:1, :], (256, 128))
 
 
 def inverse_kernel(in_ref, fourier_ref, real_ref, twist_ref, out_ref, energy_ref):
     def get(h, part):
-        return in_ref[128 * h : 128 * h + 128, 128 * part : 128 * part + 128]
+        return in_ref[pl.ds(384 * h + part, 128, stride=3), :]
 
     def put(a, value):
         out_ref[0, :, 128 * a : 128 * a + 128] = value[:16]
@@ -298,25 +296,31 @@
     inverse_y(
         get, (fourier_ref[0], fourier_ref[1]), (real_ref[0], real_ref[1]), twist_ref[...], put
     )
-    energy_ref[...] = jnp.sum(in_ref[:, 256:384], keepdims=True) * (1.0 / CELLS)
+    energy_ref[...] = jnp.sum(in_ref[pl.ds(2, 256, stride=3), :], keepdims=True) * (1.0 / CELLS)
+
+
+def exchange(rows):
+    width = rows.shape[0] // 256
+    message = rows.reshape(256, 1, 128 * width)
+    return lax.all_to_all(message, ALL, split_axis=0, concat_axis=0, tiled=True).reshape(rows.shape)
 
 
 def per_device(concentration):
     whole = pl.BlockSpec(memory_space=pltpu.VMEM)
     outgoing, bulk = pl.pallas_call(
         forward_kernel,
-        out_shape=(jax.ShapeDtypeStruct((256, 512), f32), jax.ShapeDtypeStruct((8, 128), f32)),
+        out_shape=(jax.ShapeDtypeStruct((1024, 128), f32), jax.ShapeDtypeStruct((8, 128), f32)),
         in_specs=[whole] * 4,
         out_specs=(whole, whole),
     )(concentration, FOURIER, REAL, Y_TWIST)
-    columns = lax.all_to_all(outgoing, ALL, split_axis=0, concat_axis=0, tiled=True)
+    columns = exchange(outgoing)
     leaving = pl.pallas_call(
         middle_kernel,
-        out_shape=jax.ShapeDtypeStruct((256, 384), f32),
+        out_shape=jax.ShapeDtypeStruct((768, 128), f32),
         in_specs=[whole] * 5,
         out_specs=whole,
     )(columns, bulk, FOURIER, LANES, X_TWIST)
-    rows_back = lax.all_to_all(leaving, ALL, split_axis=0, concat_axis=0, tiled=True)
+    rows_back = exchange(leaving)
     new_field, energy = pl.pallas_call(
         inverse_kernel,
         out_shape=(jax.ShapeDtypeStruct(concentration.shape, f32), jax.ShapeDtypeStruct((1, 1), f32)),

time: 74.6 us -> 71.8 us (0.962)
  local copies, waits for them, and re-layouts: 4.56 us -> 0 us
  blocking collectives: 60.2 us -> 62.1 us
    all_to_all x2 -> x0, local copies, waits for them, and re-layouts: 2.98 us -> none  [the longest x1 1.58 us: per_device(): lax.all_to_all(outgoing, ALL, split_axis=0, concat_axis=0, tiled=True)]
    all_to_all x2, blocking collectives: 60.2 us -> 62.1 us  [exchange(): lax.all_to_all(message, ALL, split_axis=0, concat_axis=0, tiled=True)]
    unnamed x2 -> x0, local copies, waits for them, and re-layouts: 1.58 us -> none
where the time goes in v1:
time: 71.8 us; the launch traced here: 71.6 us
  blocking collectives  62.1 us (86%)
  Pallas kernels  8.89 us (12%)
    all_to_all x2, blocking collectives, exchange(): lax.all_to_all(message, ALL, split_axis=0, concat_axis=0, tiled=True)  62.1 us
    pallas_call x1, Pallas kernels, per_device(): pl.pallas_call(middle_kernel, out_shape=jax.ShapeDtypeStruct((768, 128),...  3.87 us
    pallas_call x1, Pallas kernels, per_device(): pl.pallas_call(forward_kernel, out_shape=(jax.ShapeDtypeStruct((1024, 128...  2.73 us
    pallas_call x1, Pallas kernels, per_device(): pl.pallas_call(inverse_kernel, out_shape=(jax.ShapeDtypeStruct(concentrat...  2.29 us

profile of v1, /device:TPU:1, one launch (start us, length us, event | category | flops | bytes accessed | tf_op | source)
XLA Modules:
  0.0 71.6 jit_solution(8192264298137194405)
XLA Ops:
  0.6 2.7 %shard_map.77 = (f32[1024,128]{1,0:T(8,128)}, f32[8,128]{1,0:T(8,128)}) custom-call(f32[2,16,2048]{2,1,0:T(8,128)} %c_ref.1, bf16[2,256,256]{2,1,0:T(8,128)(2,1)} %constant.10.clone.fourier_ref, bf16[2,256,256]{2,1,0:T(8,128)(2,1)} %constant.11.clone.real_ref, f32[16,128]{1,0:T(8,128)} %constant.12.clone.twist_ref), custom_call_target="tpu_custom_call" | custom-call | tf_op jit(solution)/shard_map/pallas_call | solution.py:310
  3.4 36.2 %all_to_all.10 = f32[256,1,512]{2,1,0:T(1,128)} all-to-all(f32[256,1,512]{2,1,0:T(1,128)} %bitcast.8), channel_id=1, replica_groups=mesh['section'=2,'slab'=128] {'section','slab'}, dimensions={0} | all-to-all | bytes 1048576 | tf_op jit(solution)/shard_map/all_to_all | solution.py:305
  39.5 3.9 %shard_map.78 = f32[768,128]{1,0:T(8,128)} custom-call(f32[1024,128]{1,0:T(8,128)} %bitcast.5, f32[8,128]{1,0:T(8,128)} %get-tuple-element.7.bulk_ref, bf16[2,256,256]{2,1,0:T(8,128)(2,1)} %constant.10.clone.fourier_ref, bf16[2,2,256,256]{3,2,1,0:T(8,128)(2,1)} %constant.13.clone.lanes_ref, f32[2,128,128]{2,1,0:T(8,128)} %constant.14.clone.twist_ref), custom_call_target="tpu_custom_call" | custom-call | tf_op jit(solution)/shard_map/pallas_call | solution.py:317
  43.4 25.9 %all_to_all.11 = f32[256,1,384]{2,1,0:T(1,128)} all-to-all(f32[256,1,384]{2,1,0:T(1,128)} %bitcast.7), channel_id=1, replica_groups=mesh['section'=2,'slab'=128] {'section','slab'}, dimensions={0} | all-to-all | bytes 786432 | tf_op jit(solution)/shard_map/all_to_all | solution.py:305
  69.3 2.3 %shard_map.79 = (f32[2,16,2048]{2,1,0:T(8,128)}, f32[1,1]{1,0:T(1,128)}) custom-call(f32[768,128]{1,0:T(8,128)} %bitcast.6, bf16[2,256,256]{2,1,0:T(8,128)(2,1)} %constant.10.clone.fourier_ref, bf16[2,256,256]{2,1,0:T(8,128)(2,1)} %constant.11.clone.real_ref, f32[16,128]{1,0:T(8,128)} %constant.12.clone.twist_ref), custom_call_target="tpu_custom_call" | custom-call | tf_op jit(solution)/shard_map/pallas_call | solution.py:324

commit v2 on v1

--- a/solution.py
+++ b/solution.py
@@ -99,7 +99,7 @@
     return total
 
 
-def y_slots(field, twist):
+def y_slots(field):
     at = [field[:, 128 * a : 128 * a + 128] for a in range(16)]
     add = [at[a] + at[a + 8] for a in range(8)]
     sub = [at[a] - at[a + 8] for a in range(8)]
@@ -115,20 +115,23 @@
     for j in (1, 3, 5, 7):
         real[j] = weighted([(1.0, sub[0])] + [(COS16[j * a % 16], minus[a]) for a in (1, 2, 3)])
         imag[j] = weighted([(-SIN16[j * a % 16], plus[a]) for a in (1, 2, 3, 4)])
-    for j in range(1, 8):
-        cos, sin = twist[j : j + 1], twist[8 + j : 9 + j]
-        slots.append(
-            jnp.concatenate([real[j] * cos + imag[j] * sin, imag[j] * cos - real[j] * sin], 1)
-        )
-    return slots
-
-
-def forward_y(field, fourier, real_rows, twist, put):
+    return slots + [(real[j], imag[j]) for j in range(1, 8)]
+
+
+def forward_y(field, read_fourier, read_real, read_twist, put):
     squared = field * field
     bulk = squared * (0.25 * squared - 0.5)
     cubic = squared * field - field
-    for f, value in ((0, field), (1, cubic)):
-        slots = y_slots(value, twist)
+    both = [y_slots(field), y_slots(cubic)]
+    twist = read_twist()
+    for slots in both:
+        for j in range(1, 8):
+            real, imag = slots[j]
+            cos, sin = twist[j : j + 1], twist[8 + j : 9 + j]
+            slots[j] = jnp.concatenate([real * cos + imag * sin, imag * cos - real * sin], 1)
+    real_rows = read_real()
+    fourier = read_fourier()
+    for f, slots in enumerate(both):
         first = product(real_rows, split(slots[0]), NT)
         for h in (0, 1):
             rows = jnp.concatenate(slots[4 * h : 4 * h + 4], 0)
@@ -255,14 +258,31 @@
         put(a + 8, even[a] - odd[a])
 
 
-def forward_kernel(c_ref, fourier_ref, real_ref, twist_ref, out_ref, bulk_ref):
+def forward_kernel(
+    c_hbm, fourier_hbm, real_hbm, twist_hbm, out_ref, bulk_ref, c_ref, fourier_ref, real_ref, twist_ref, sems
+):
+    sources = (c_hbm, twist_hbm, real_hbm, fourier_hbm)
+    targets = (c_ref, twist_ref, real_ref, fourier_ref)
+    copies = [
+        pltpu.make_async_copy(source, target, sems.at[n])
+        for n, (source, target) in enumerate(zip(sources, targets))
+    ]
+    for copy in copies:
+        copy.start()
+
     def put(h, part, f, value):
         out_ref[pl.ds(512 * h + 2 * part + f, 128, stride=4), :] = value
 
+    def late(n, ref):
+        def read():
+            copies[n].wait()
+            return ref[...]
+
+        return read
+
+    copies[0].wait()
     field = jnp.concatenate([c_ref[0], c_ref[1]], 0)
-    lanes = forward_y(
-        field, (fourier_ref[0], fourier_ref[1]), (real_ref[0], real_ref[1]), twist_ref[...], put
-    )
+    lanes = forward_y(field, late(3, fourier_ref), late(2, real_ref), late(1, twist_ref), put)
     bulk_ref[...] = jnp.broadcast_to(jnp.sum(lanes, 0, keepdims=True), (8, 128))
 
 
@@ -307,11 +327,20 @@
 
 def per_device(concentration):
     whole = pl.BlockSpec(memory_space=pltpu.VMEM)
+    params = pltpu.CompilerParams(vmem_limit_bytes=12 << 20)
     outgoing, bulk = pl.pallas_call(
         forward_kernel,
         out_shape=(jax.ShapeDtypeStruct((1024, 128), f32), jax.ShapeDtypeStruct((8, 128), f32)),
-        in_specs=[whole] * 4,
+        in_specs=[pl.BlockSpec(memory_space=pltpu.HBM)] * 4,
         out_specs=(whole, whole),
+        scratch_shapes=[
+            pltpu.VMEM(concentration.shape, f32),
+            pltpu.VMEM(FOURIER.shape, bf16),
+            pltpu.VMEM(REAL.shape, bf16),
+            pltpu.VMEM(Y_TWIST.shape, f32),
+            pltpu.SemaphoreType.DMA((4,)),
+        ],
+        compiler_params=params,
     )(concentration, FOURIER, REAL, Y_TWIST)
     columns = exchange(outgoing)
     leaving = pl.pallas_call(
@@ -319,6 +348,7 @@
         out_shape=jax.ShapeDtypeStruct((768, 128), f32),
         in_specs=[whole] * 5,
         out_specs=whole,
+        compiler_params=params,
     )(columns, bulk, FOURIER, LANES, X_TWIST)
     rows_back = exchange(leaving)
     new_field, energy = pl.pallas_call(
@@ -326,6 +356,7 @@
         out_shape=(jax.ShapeDtypeStruct(concentration.shape, f32), jax.ShapeDtypeStruct((1, 1), f32)),
         in_specs=[whole] * 4,
         out_specs=(whole, whole),
+        compiler_params=params,
     )(rows_back, FOURIER, REAL, Y_TWIST)
     return new_field, energy.reshape(())
 

time: 71.8 us -> 69.1 us (0.962)
  Pallas kernels: 8.89 us -> 4.15 us
  local copies, waits for them, and re-layouts: 0 us -> 3.58 us
  blocking collectives: 62.1 us -> 60.4 us
    unnamed x0 -> x18, local copies, waits for them, and re-layouts: none -> 3.58 us
    pallas_call x1, Pallas kernels: 3.87 us -> 1.83 us  [per_device(): pl.pallas_call(middle_kernel, out_shape=jax.ShapeDtypeStruct((768, 128),...]
    all_to_all x2, blocking collectives: 62.1 us -> 60.4 us  [exchange(): lax.all_to_all(message, ALL, split_axis=0, concat_axis=0, tiled=True)]
    pallas_call x1, Pallas kernels: 2.73 us -> 1.18 us  [per_device(): pl.pallas_call(forward_kernel, out_shape=(jax.ShapeDtypeStruct((1024, 128...]
    pallas_call x1, Pallas kernels: 2.29 us -> 1.14 us  [per_device(): pl.pallas_call(inverse_kernel, out_shape=(jax.ShapeDtypeStruct(concentrat...]
where the time goes in v2:
time: 69.1 us; the launch traced here: 68.8 us
  blocking collectives  60.4 us (87%)
  Pallas kernels  4.15 us (6%)
  local copies, waits for them, and re-layouts  3.58 us (5%)
  between operations  0.7 us (1%)
    all_to_all x2, blocking collectives, exchange(): lax.all_to_all(message, ALL, split_axis=0, concat_axis=0, tiled=True)  60.4 us
    unnamed x18, local copies, waits for them, and re-layouts  3.58 us
    pallas_call x1, Pallas kernels, per_device(): pl.pallas_call(middle_kernel, out_shape=jax.ShapeDtypeStruct((768, 128),...  1.83 us

profile of v2, /device:TPU:1, one launch (start us, length us, event | category | flops | bytes accessed | tf_op | source)
XLA Modules:
  0.0 68.8 jit_solution(11580113141874126415)
XLA Ops:
  0.6 0.0 copy-start
  0.6 0.9 %copy-done = bf16[2,256,256]{2,1,0:T(8,128)(2,1)S(1)} copy-done((bf16[2,256,256]{2,1,0:T(8,128)(2,1)S(1)}, bf16[2,256,256]{2,1,0:T(8,128)(2,1)}, u32[]{:S(2)}) %copy-start) | copy-done | bytes 262168
  1.6 0.0 copy-start.2
  1.6 0.9 %copy-done.2 = bf16[2,256,256]{2,1,0:T(8,128)(2,1)S(1)} copy-done((bf16[2,256,256]{2,1,0:T(8,128)(2,1)S(1)}, bf16[2,256,256]{2,1,0:T(8,128)(2,1)}, u32[]{:S(2)}) %copy-start.2) | copy-done | bytes 262168
  2.5 0.0 copy-start.5
  2.5 0.9 %copy-done.5 = f32[2,16,2048]{2,1,0:T(8,128)S(1)} copy-done((f32[2,16,2048]{2,1,0:T(8,128)S(1)}, f32[2,16,2048]{2,1,0:T(8,128)}, u32[]{:S(2)}) %copy-start.5) | copy-done | bytes 262168
  3.5 0.0 copy-start.7
  3.5 0.7 %copy-done.7 = f32[16,128]{1,0:T(8,128)S(1)} copy-done((f32[16,128]{1,0:T(8,128)S(1)}, f32[16,128]{1,0:T(8,128)}, u32[]{:S(2)}) %copy-start.7) | copy-done | bytes 8216
  4.2 1.2 %shard_map.77 = (f32[1024,128]{1,0:T(8,128)S(1)}, f32[8,128]{1,0:T(8,128)S(1)}) custom-call(f32[2,16,2048]{2,1,0:T(8,128)S(1)} %copy-done.5, bf16[2,256,256]{2,1,0:T(8,128)(2,1)S(1)} %copy-done, bf16[2,256,256]{2,1,0:T(8,128)(2,1)S(1)} %copy-done.2, f32[16,128]{1,0:T(8,128)S(1)} %copy-done.7), custom_call_target="tpu_custom_call" | custom-call | tf_op jit(solution)/shard_map/pallas_call | solution.py:331
  5.4 0.0 copy-start.1
  5.4 0.0 copy-start.4
  5.4 0.0 copy-start.6
  5.4 35.8 %all_to_all.10 = f32[256,1,512]{2,1,0:T(1,128)S(1)} all-to-all(f32[256,1,512]{2,1,0:T(1,128)S(1)} %bitcast.8), channel_id=1, replica_groups=mesh['section'=2,'slab'=128] {'section','slab'}, dimensions={0} | all-to-all | bytes 1048576 | tf_op jit(solution)/shard_map/all_to_all | solution.py:325
  41.3 0.0 copy-done.1
  41.3 0.0 copy-done.4
  41.3 0.0 copy-done.6
  41.3 1.8 %shard_map.78 = f32[768,128]{1,0:T(8,128)S(1)} custom-call(f32[1024,128]{1,0:T(8,128)S(1)} %bitcast.5, f32[8,128]{1,0:T(8,128)S(1)} %get-tuple-element.7.bulk_ref, bf16[2,256,256]{2,1,0:T(8,128)(2,1)S(1)} %copy-done.1, bf16[2,2,256,256]{3,2,1,0:T(8,128)(2,1)S(1)} %copy-done.4, f32[2,128,128]{2,1,0:T(8,128)S(1)} %copy-done.6), custom_call_target="tpu_custom_call" | custom-call | tf_op jit(solution)/shard_map/pallas_call | solution.py:346
  43.1 0.0 copy-start.3
  43.1 0.0 copy-start.8
  43.1 24.5 %all_to_all.11 = f32[256,1,384]{2,1,0:T(1,128)S(1)} all-to-all(f32[256,1,384]{2,1,0:T(1,128)S(1)} %bitcast.7), channel_id=1, replica_groups=mesh['section'=2,'slab'=128] {'section','slab'}, dimensions={0} | all-to-all | bytes 786432 | tf_op jit(solution)/shard_map/all_to_all | solution.py:325
  67.6 0.0 copy-done.3
  67.6 0.0 copy-done.8
  67.6 1.1 %shard_map.79 = (f32[2,16,2048]{2,1,0:T(8,128)}, f32[1,1]{1,0:T(1,128)}) custom-call(f32[768,128]{1,0:T(8,128)S(1)} %bitcast.6, bf16[2,256,256]{2,1,0:T(8,128)(2,1)S(1)} %copy-done.1, bf16[2,256,256]{2,1,0:T(8,128)(2,1)S(1)} %copy-done.3, f32[16,128]{1,0:T(8,128)S(1)} %copy-done.8), custom_call_target="tpu_custom_call" | custom-call | tf_op jit(solution)/shard_map/pallas_call | solution.py:354
Async XLA Ops:
  0.6 1.0 %copy-start = (bf16[2,256,256]{2,1,0:T(8,128)(2,1)S(1)}, bf16[2,256,256]{2,1,0:T(8,128)(2,1)}, u32[]{:S(2)}) copy-start(bf16[2,256,256]{2,1,0:T(8,128)(2,1)} %constant.10.clone.fourier_hbm.fourier_ref) | copy-start | bytes 786436
  1.6 0.9 %copy-start.2 = (bf16[2,256,256]{2,1,0:T(8,128)(2,1)S(1)}, bf16[2,256,256]{2,1,0:T(8,128)(2,1)}, u32[]{:S(2)}) copy-start(bf16[2,256,256]{2,1,0:T(8,128)(2,1)} %constant.11.clone.real_hbm.real_ref) | copy-start | bytes 786436
  2.5 0.9 %copy-start.5 = (f32[2,16,2048]{2,1,0:T(8,128)S(1)}, f32[2,16,2048]{2,1,0:T(8,128)}, u32[]{:S(2)}) copy-start(f32[2,16,2048]{2,1,0:T(8,128)} %c_hbm.1) | copy-start | bytes 786436
  3.5 0.7 %copy-start.7 = (f32[16,128]{1,0:T(8,128)S(1)}, f32[16,128]{1,0:T(8,128)}, u32[]{:S(2)}) copy-start(f32[16,128]{1,0:T(8,128)} %constant.12.clone.twist_hbm.twist_ref) | copy-start | bytes 24580
  5.4 35.9 %copy-start.1 = (bf16[2,256,256]{2,1,0:T(8,128)(2,1)S(1)}, bf16[2,256,256]{2,1,0:T(8,128)(2,1)}, u32[]{:S(2)}) copy-start(bf16[2,256,256]{2,1,0:T(8,128)(2,1)} %constant.10.clone.fourier_hbm.fourier_ref) | copy-start | bytes 786436
  5.4 35.9 %copy-start.4 = (bf16[2,2,256,256]{3,2,1,0:T(8,128)(2,1)S(1)}, bf16[2,2,256,256]{3,2,1,0:T(8,128)(2,1)}, u32[]{:S(2)}) copy-start(bf16[2,2,256,256]{3,2,1,0:T(8,128)(2,1)} %constant.13.clone.lanes_ref) | copy-start | bytes 1572868
  5.4 35.9 %copy-start.6 = (f32[2,128,128]{2,1,0:T(8,128)S(1)}, f32[2,128,128]{2,1,0:T(8,128)}, u32[]{:S(2)}) copy-start(f32[2,128,128]{2,1,0:T(8,128)} %constant.14.clone.twist_ref) | copy-start | bytes 393220
  43.1 24.5 %copy-start.3 = (bf16[2,256,256]{2,1,0:T(8,128)(2,1)S(1)}, bf16[2,256,256]{2,1,0:T(8,128)(2,1)}, u32[]{:S(2)}) copy-start(bf16[2,256,256]{2,1,0:T(8,128)(2,1)} %constant.11.clone.real_hbm.real_ref) | copy-start | bytes 786436
  43.1 24.5 %copy-start.8 = (f32[16,128]{1,0:T(8,128)S(1)}, f32[16,128]{1,0:T(8,128)}, u32[]{:S(2)}) copy-start(f32[16,128]{1,0:T(8,128)} %constant.12.clone.twist_hbm.twist_ref) | copy-start | bytes 24580

commit v3 on v2

--- a/solution.py
+++ b/solution.py
@@ -330,7 +330,7 @@
     params = pltpu.CompilerParams(vmem_limit_bytes=12 << 20)
     outgoing, bulk = pl.pallas_call(
         forward_kernel,
-        out_shape=(jax.ShapeDtypeStruct((1024, 128), f32), jax.ShapeDtypeStruct((8, 128), f32)),
+        out_shape=(pltpu.VMEM((1024, 128), f32), pltpu.VMEM((8, 128), f32)),
         in_specs=[pl.BlockSpec(memory_space=pltpu.HBM)] * 4,
         out_specs=(whole, whole),
         scratch_shapes=[
@@ -341,7 +341,7 @@
             pltpu.SemaphoreType.DMA((4,)),
         ],
         compiler_params=params,
-    )(concentration, FOURIER, REAL, Y_TWIST)
+    )(*[pltpu.with_memory_space_constraint(a, pltpu.HBM) for a in (concentration, FOURIER, REAL, Y_TWIST)])
     columns = exchange(outgoing)
     leaving = pl.pallas_call(
         middle_kernel,

time: 69.1 us -> 66.3 us (0.959)
  local copies, waits for them, and re-layouts: 3.58 us -> 0.03 us
  Pallas kernels: 4.15 us -> 5.04 us
    unnamed x18 -> x10, local copies, waits for them, and re-layouts: 3.58 us -> 0.03 us
    pallas_call x1, Pallas kernels: 1.18 us -> 2.07 us  [per_device(): pl.pallas_call(forward_kernel, out_shape=(pltpu.VMEM((1024, 128), f32), p...]
where the time goes in v3:
time: 66.3 us; the launch traced here: 66.1 us
  blocking collectives  60.4 us (91%)
  Pallas kernels  5.04 us (8%)
  between operations  0.69 us (1%)
    all_to_all x2, blocking collectives, exchange(): lax.all_to_all(message, ALL, split_axis=0, concat_axis=0, tiled=True)  60.4 us
    pallas_call x1, Pallas kernels, per_device(): pl.pallas_call(forward_kernel, out_shape=(pltpu.VMEM((1024, 128), f32), p...  2.07 us
    pallas_call x1, Pallas kernels, per_device(): pl.pallas_call(middle_kernel, out_shape=jax.ShapeDtypeStruct((768, 128),...  1.83 us

profile of v3, /device:TPU:1, one launch (start us, length us, event | category | flops | bytes accessed | tf_op | source)
XLA Modules:
  0.0 66.1 jit_solution(8480559004344642828)
XLA Ops:
  0.6 2.1 %shard_map.77 = (f32[1024,128]{1,0:T(8,128)S(1)}, f32[8,128]{1,0:T(8,128)S(1)}) custom-call(f32[2,16,2048]{2,1,0:T(8,128)} %c_hbm.1, bf16[2,256,256]{2,1,0:T(8,128)(2,1)} %constant.10.clone.fourier_hbm.fourier_ref, bf16[2,256,256]{2,1,0:T(8,128)(2,1)} %constant.11.clone.real_hbm.real_ref, f32[16,128]{1,0:T(8,128)} %constant.12.clone.twist_hbm.twist_ref), custom_call_target="tpu_custom_call" | custom-call | tf_op jit(solution)/shard_map/pallas_call | solution.py:331
  2.7 0.0 copy-start
  2.7 0.0 copy-start.2
  2.7 0.0 copy-start.3
  2.7 35.9 %all_to_all.10 = f32[256,1,512]{2,1,0:T(1,128)S(1)} all-to-all(f32[256,1,512]{2,1,0:T(1,128)S(1)} %bitcast.8), channel_id=1, replica_groups=mesh['section'=2,'slab'=128] {'section','slab'}, dimensions={0} | all-to-all | bytes 1048576 | tf_op jit(solution)/shard_map/all_to_all | solution.py:325
  38.6 0.0 copy-done
  38.6 0.0 copy-done.2
  38.6 0.0 copy-done.3
  38.6 1.8 %shard_map.78 = f32[768,128]{1,0:T(8,128)S(1)} custom-call(f32[1024,128]{1,0:T(8,128)S(1)} %bitcast.5, f32[8,128]{1,0:T(8,128)S(1)} %get-tuple-element.7.bulk_ref, bf16[2,256,256]{2,1,0:T(8,128)(2,1)S(1)} %copy-done, bf16[2,2,256,256]{3,2,1,0:T(8,128)(2,1)S(1)} %copy-done.2, f32[2,128,128]{2,1,0:T(8,128)S(1)} %copy-done.3), custom_call_target="tpu_custom_call" | custom-call | tf_op jit(solution)/shard_map/pallas_call | solution.py:346
  40.4 0.0 copy-start.1
  40.5 0.0 copy-start.4
  40.5 24.5 %all_to_all.11 = f32[256,1,384]{2,1,0:T(1,128)S(1)} all-to-all(f32[256,1,384]{2,1,0:T(1,128)S(1)} %bitcast.7), channel_id=1, replica_groups=mesh['section'=2,'slab'=128] {'section','slab'}, dimensions={0} | all-to-all | bytes 786432 | tf_op jit(solution)/shard_map/all_to_all | solution.py:325
  65.0 0.0 copy-done.1
  65.0 0.0 copy-done.4
  65.0 1.1 %shard_map.79 = (f32[2,16,2048]{2,1,0:T(8,128)}, f32[1,1]{1,0:T(1,128)}) custom-call(f32[768,128]{1,0:T(8,128)S(1)} %bitcast.6, bf16[2,256,256]{2,1,0:T(8,128)(2,1)S(1)} %copy-done, bf16[2,256,256]{2,1,0:T(8,128)(2,1)S(1)} %copy-done.1, f32[16,128]{1,0:T(8,128)S(1)} %copy-done.4), custom_call_target="tpu_custom_call" | custom-call | tf_op jit(solution)/shard_map/pallas_call | solution.py:354
Async XLA Ops:
  2.7 35.9 %copy-start = (bf16[2,256,256]{2,1,0:T(8,128)(2,1)S(1)}, bf16[2,256,256]{2,1,0:T(8,128)(2,1)}, u32[]{:S(2)}) copy-start(bf16[2,256,256]{2,1,0:T(8,128)(2,1)} %constant.10.clone.fourier_hbm.fourier_ref) | copy-start | bytes 786436
  2.7 35.9 %copy-start.2 = (bf16[2,2,256,256]{3,2,1,0:T(8,128)(2,1)S(1)}, bf16[2,2,256,256]{3,2,1,0:T(8,128)(2,1)}, u32[]{:S(2)}) copy-start(bf16[2,2,256,256]{3,2,1,0:T(8,128)(2,1)} %constant.13.clone.lanes_ref) | copy-start | bytes 1572868
  2.7 35.9 %copy-start.3 = (f32[2,128,128]{2,1,0:T(8,128)S(1)}, f32[2,128,128]{2,1,0:T(8,128)}, u32[]{:S(2)}) copy-start(f32[2,128,128]{2,1,0:T(8,128)} %constant.14.clone.twist_ref) | copy-start | bytes 393220
  40.4 24.5 %copy-start.1 = (bf16[2,256,256]{2,1,0:T(8,128)(2,1)S(1)}, bf16[2,256,256]{2,1,0:T(8,128)(2,1)}, u32[]{:S(2)}) copy-start(bf16[2,256,256]{2,1,0:T(8,128)(2,1)} %constant.11.clone.real_hbm.real_ref) | copy-start | bytes 786436
  40.5 24.5 %copy-start.4 = (f32[16,128]{1,0:T(8,128)S(1)}, f32[16,128]{1,0:T(8,128)}, u32[]{:S(2)}) copy-start(f32[16,128]{1,0:T(8,128)} %constant.12.clone.twist_hbm.twist_ref) | copy-start | bytes 24580

commit v4 on v3

--- a/solution.py
+++ b/solution.py
@@ -7,9 +7,11 @@
 from jax import lax
 from jax.experimental import pallas as pl
 from jax.experimental.pallas import tpu as pltpu
+from jax.sharding import Mesh
 from jax.sharding import PartitionSpec as P
 
-ALL = ("section", "slab")
+SLAB = ("slab_y", "slab_x", "slab_z", "slab_core")
+ALL = ("section", "slab_z", "slab_y", "slab_x", "slab_core")
 NX = 2048
 NY = 2048
 NZ = 4
@@ -33,6 +35,10 @@
     return halves(np.block([[np.cos(angle), np.sin(angle)], [-np.sin(angle), np.cos(angle)]]))
 
 
+def slab_order():
+    return np.arange(128).reshape(4, 2, 8, 2).transpose(2, 0, 1, 3).reshape(128)
+
+
 def real_table():
     angle = 2.0 * np.pi * (np.outer(np.arange(128), np.arange(256)) % 256) / 256
     lower = -np.sin(angle)
@@ -60,6 +66,9 @@
 
 
 FOURIER = fourier_table()
+ORDER = slab_order()
+GATHER = FOURIER[:, :, np.concatenate([ORDER, 128 + ORDER])]
+SPREAD = FOURIER[:, ORDER, :]
 REAL = real_table()
 LANES = np.stack([lane_table(0), lane_table(1)])
 Y_TWIST = y_twist_table()
@@ -158,10 +167,10 @@
     return numerator * inverse, time_step * wave_sq * inverse
 
 
-def middle(get, section_at, slab_at, fourier, lanes, twist, put):
+def middle(get, section_at, lane_at, gather, lanes, spread_table, twist, put):
     lane = lax.broadcasted_iota(jnp.int32, (128, 128), 1)
     row = lax.broadcasted_iota(jnp.int32, (128, 128), 0)
-    packed = (lane < 32) & (section_at == 0) & (slab_at == 0)
+    packed = (lane < 32) & (section_at == 0) & (lane_at == 0)
     cos, sin = twist[0], twist[1]
     parts = []
     for s in (0, 1):
@@ -177,14 +186,14 @@
             )
         )
     slot = 4 * section_at + lane // 32
-    y_index = jnp.where(slot == 0, 8 * slab_at, slot + 16 * slab_at)
+    y_index = jnp.where(slot == 0, 8 * lane_at, slot + 16 * lane_at)
     x_index = row + 128 * (lane % 16)
     wave_x = wave_square(x_index, NX)
     wave_xy = wave_x + wave_square(y_index, NY)
     half_y = (2.0 * math.pi / NY * (NY // 2)) ** 2
     back = []
     for sigma in (0, 1):
-        spread = product(fourier, split(stacked[sigma]), NN)
+        spread = product(gather, split(stacked[sigma]), NN)
         rows = []
         for f in (0, 1):
             re, im = spread[:128, 128 * f : 128 * f + 128], spread[128:, 128 * f : 128 * f + 128]
@@ -212,9 +221,7 @@
         (m_re, m_im), (s_re, s_im) = both
         upper = jnp.concatenate([m_re, jnp.where(packed, s_re, m_im)], 1)
         lower = jnp.concatenate([-m_im, jnp.where(packed, -s_im, m_re)], 1)
-        out = product(
-            (fourier[0][:128], fourier[1][:128]), split(jnp.concatenate([upper, lower], 0)), NN
-        )
+        out = product(spread_table, split(jnp.concatenate([upper, lower], 0)), NN)
         put(s, 0, out[:, :128])
         put(s, 1, out[:, 128:])
 
@@ -286,7 +293,7 @@
     bulk_ref[...] = jnp.broadcast_to(jnp.sum(lanes, 0, keepdims=True), (8, 128))
 
 
-def middle_kernel(in_ref, bulk_ref, fourier_ref, lanes_ref, twist_ref, out_ref):
+def middle_kernel(in_ref, bulk_ref, gather_ref, lanes_ref, spread_ref, twist_ref, out_ref):
     def get(s, part, f):
         return in_ref[pl.ds(512 * s + 2 * part + f, 128, stride=4), :]
 
@@ -296,9 +303,13 @@
     middle(
         get,
         lax.axis_index("section"),
-        lax.axis_index("slab"),
-        (fourier_ref[0], fourier_ref[1]),
+        16 * lax.axis_index("slab_z")
+        + 4 * lax.axis_index("slab_y")
+        + 2 * lax.axis_index("slab_x")
+        + lax.axis_index("slab_core"),
+        (gather_ref[0], gather_ref[1]),
         lanes_ref,
+        (spread_ref[0], spread_ref[1]),
         twist_ref,
         put,
     )
@@ -346,10 +357,10 @@
     leaving = pl.pallas_call(
         middle_kernel,
         out_shape=jax.ShapeDtypeStruct((768, 128), f32),
-        in_specs=[whole] * 5,
+        in_specs=[whole] * 6,
         out_specs=whole,
         compiler_params=params,
-    )(columns, bulk, FOURIER, LANES, X_TWIST)
+    )(columns, bulk, GATHER, LANES, SPREAD, X_TWIST)
     rows_back = exchange(leaving)
     new_field, energy = pl.pallas_call(
         inverse_kernel,
@@ -362,10 +373,11 @@
 
 
 def solution(mesh):
+    finer = Mesh(mesh.devices.reshape(2, 4, 2, 8, 2), ("section",) + SLAB)
     return jax.shard_map(
         per_device,
-        mesh=mesh,
-        in_specs=(P("section", "slab", None),),
-        out_specs=(P("section", "slab", None), P()),
+        mesh=finer,
+        in_specs=(P("section", SLAB, None),),
+        out_specs=(P("section", SLAB, None), P()),
         check_vma=False,
     )

time: 66.3 us -> 66.1 us (level)
  no operation moved by 1% of the time
where the time goes in v4:
time: 66.1 us; the launch traced here: 66 us
  blocking collectives  60.2 us (91%)
  Pallas kernels  5.05 us (8%)
  between operations  0.72 us (1%)
    all_to_all x2, blocking collectives, exchange(): lax.all_to_all(message, ALL, split_axis=0, concat_axis=0, tiled=True)  60.2 us
    pallas_call x1, Pallas kernels, per_device(): pl.pallas_call(forward_kernel, out_shape=(pltpu.VMEM((1024, 128), f32), p...  2.07 us
    pallas_call x1, Pallas kernels, per_device(): pl.pallas_call(middle_kernel, out_shape=jax.ShapeDtypeStruct((768, 128),...  1.84 us

profile of v4, /device:TPU:1, one launch (start us, length us, event | category | flops | bytes accessed | tf_op | source)
XLA Modules:
  0.0 66.0 jit_solution(9244826143024048999)
XLA Ops:
  0.6 2.1 %shard_map.95 = (f32[1024,128]{1,0:T(8,128)S(1)}, f32[8,128]{1,0:T(8,128)S(1)}) custom-call(f32[2,16,2048]{2,1,0:T(8,128)} %c_hbm.1, bf16[2,256,256]{2,1,0:T(8,128)(2,1)} %constant.14.clone.fourier_hbm.fourier_ref, bf16[2,256,256]{2,1,0:T(8,128)(2,1)} %constant.15.clone.real_hbm.real_ref, f32[16,128]{1,0:T(8,128)} %constant.16.clone.twist_hbm.twist_ref), custom_call_target="tpu_custom_call" | custom-call | tf_op jit(solution)/shard_map/pallas_call | solution.py:342
  2.7 0.0 copy-start.2
  2.7 0.0 copy-start.3
  2.7 0.0 copy-start.4
  2.7 0.0 copy-start.5
  2.8 36.3 %all_to_all.10 = f32[256,1,512]{2,1,0:T(1,128)S(1)} all-to-all(f32[256,1,512]{2,1,0:T(1,128)S(1)} %bitcast.8), channel_id=1, replica_groups=mesh['section'=2,'slab_y'=4,'slab_x'=2,'slab_z'=8,'slab_core'=2] {'secti..., dimensions={0} | all-to-all | bytes 1048576 | tf_op jit(solution)/shard_map/all_to_all | solution.py:336
  39.1 0.0 copy-done.2
  39.1 0.0 copy-done.3
  39.1 0.0 copy-done.4
  39.1 0.0 copy-done.5
  39.1 1.8 %shard_map.96 = f32[768,128]{1,0:T(8,128)S(1)} custom-call(f32[1024,128]{1,0:T(8,128)S(1)} %bitcast.5, f32[8,128]{1,0:T(8,128)S(1)} %get-tuple-element.7.bulk_ref, bf16[2,256,256]{2,1,0:T(8,128)(2,1)S(1)} %copy-done.3, bf16[2,2,256,256]{3,2,1,0:T(8,128)(2,1)S(1)} %copy-done.2, bf16[2,128,256]{2,1,0:T(8,128)(2,1)S(1)} %copy-done.5, f32[2,128,128]{2,1,0:T(8,128)S(1)} %copy-done.4), custom_call_target="tpu_custom_call" | custom-call | tf_op jit(solution)/shard_map/pallas_call | solution.py:357
  40.9 0.0 copy-start
  40.9 0.0 copy-start.1
  40.9 0.0 copy-start.6
  41.0 23.9 %all_to_all.11 = f32[256,1,384]{2,1,0:T(1,128)S(1)} all-to-all(f32[256,1,384]{2,1,0:T(1,128)S(1)} %bitcast.7), channel_id=1, replica_groups=mesh['section'=2,'slab_y'=4,'slab_x'=2,'slab_z'=8,'slab_core'=2] {'secti..., dimensions={0} | all-to-all | bytes 786432 | tf_op jit(solution)/shard_map/all_to_all | solution.py:336
  64.8 0.0 copy-done
  64.8 0.0 copy-done.1
  64.8 0.0 copy-done.6
  64.8 1.1 %shard_map.97 = (f32[2,16,2048]{2,1,0:T(8,128)}, f32[1,1]{1,0:T(1,128)}) custom-call(f32[768,128]{1,0:T(8,128)S(1)} %bitcast.6, bf16[2,256,256]{2,1,0:T(8,128)(2,1)S(1)} %copy-done.1, bf16[2,256,256]{2,1,0:T(8,128)(2,1)S(1)} %copy-done, f32[16,128]{1,0:T(8,128)S(1)} %copy-done.6), custom_call_target="tpu_custom_call" | custom-call | tf_op jit(solution)/shard_map/pallas_call | solution.py:365
Async XLA Ops:
  2.7 36.4 %copy-start.2 = (bf16[2,2,256,256]{3,2,1,0:T(8,128)(2,1)S(1)}, bf16[2,2,256,256]{3,2,1,0:T(8,128)(2,1)}, u32[]{:S(2)}) copy-start(bf16[2,2,256,256]{3,2,1,0:T(8,128)(2,1)} %constant.18.clone.lanes_ref) | copy-start | bytes 1572868
  2.7 36.3 %copy-start.3 = (bf16[2,256,256]{2,1,0:T(8,128)(2,1)S(1)}, bf16[2,256,256]{2,1,0:T(8,128)(2,1)}, u32[]{:S(2)}) copy-start(bf16[2,256,256]{2,1,0:T(8,128)(2,1)} %constant.17.clone.gather_ref) | copy-start | bytes 786436
  2.7 36.3 %copy-start.4 = (f32[2,128,128]{2,1,0:T(8,128)S(1)}, f32[2,128,128]{2,1,0:T(8,128)}, u32[]{:S(2)}) copy-start(f32[2,128,128]{2,1,0:T(8,128)} %constant.20.clone.twist_ref) | copy-start | bytes 393220
  2.7 36.3 %copy-start.5 = (bf16[2,128,256]{2,1,0:T(8,128)(2,1)S(1)}, bf16[2,128,256]{2,1,0:T(8,128)(2,1)}, u32[]{:S(2)}) copy-start(bf16[2,128,256]{2,1,0:T(8,128)(2,1)} %constant.19.clone.spread_ref) | copy-start | bytes 393220
  40.9 23.9 %copy-start = (bf16[2,256,256]{2,1,0:T(8,128)(2,1)S(1)}, bf16[2,256,256]{2,1,0:T(8,128)(2,1)}, u32[]{:S(2)}) copy-start(bf16[2,256,256]{2,1,0:T(8,128)(2,1)} %constant.15.clone.real_hbm.real_ref) | copy-start | bytes 786436
  40.9 23.9 %copy-start.1 = (bf16[2,256,256]{2,1,0:T(8,128)(2,1)S(1)}, bf16[2,256,256]{2,1,0:T(8,128)(2,1)}, u32[]{:S(2)}) copy-start(bf16[2,256,256]{2,1,0:T(8,128)(2,1)} %constant.14.clone.fourier_hbm.fourier_ref) | copy-start | bytes 786436
  40.9 23.9 %copy-start.6 = (f32[16,128]{1,0:T(8,128)S(1)}, f32[16,128]{1,0:T(8,128)}, u32[]{:S(2)}) copy-start(f32[16,128]{1,0:T(8,128)} %constant.16.clone.twist_hbm.twist_ref) | copy-start | bytes 24580

commit v5 on v4

--- a/solution.py
+++ b/solution.py
@@ -71,6 +71,8 @@
 SPREAD = FOURIER[:, ORDER, :]
 REAL = real_table()
 LANES = np.stack([lane_table(0), lane_table(1)])
+FOURIER_T = FOURIER.transpose(0, 2, 1)
+REAL_T = REAL.transpose(0, 2, 1)
 Y_TWIST = y_twist_table()
 X_TWIST = x_twist_table()
 COS16 = [math.cos(2.0 * math.pi * m / 16) for m in range(16)]
@@ -87,10 +89,12 @@
 
 
 def product(left, right, pattern):
-    def one(a, b):
-        return lax.dot_general(a, b, pattern, preferred_element_type=f32)
-
-    return one(left[0], right[0]) + (one(left[1], right[0]) + one(left[0], right[1]))
+    total = left[0].shape[0]
+    both = lax.dot_general(
+        jnp.concatenate(left, 0), right[0], pattern, preferred_element_type=f32
+    )
+    rest = lax.dot_general(left[0], right[1], pattern, preferred_element_type=f32)
+    return both[:total] + (both[total:] + rest)
 
 
 def weighted(terms):
@@ -139,18 +143,15 @@
             cos, sin = twist[j : j + 1], twist[8 + j : 9 + j]
             slots[j] = jnp.concatenate([real * cos + imag * sin, imag * cos - real * sin], 1)
     real_rows = read_real()
+    first = product(split(jnp.concatenate([both[0][0], both[1][0]], 0)), real_rows, NN)
     fourier = read_fourier()
-    for f, slots in enumerate(both):
-        first = product(real_rows, split(slots[0]), NT)
-        for h in (0, 1):
-            rows = jnp.concatenate(slots[4 * h : 4 * h + 4], 0)
-            out = product(fourier, split(rows), NT)
-            if h == 0:
-                lane = lax.broadcasted_iota(jnp.int32, (256, 128), 1)
-                wide = jnp.concatenate([first] * 4, 1)
-                out = jnp.where(lane < 32, wide, out)
-            put(h, 0, f, out[:128])
-            put(h, 1, f, out[128:])
+    rest = product(split(jnp.concatenate(both[0][1:] + both[1][1:], 0)), fourier, NN)
+    for f in (0, 1):
+        upper = jnp.concatenate([first[32 * f : 32 * f + 32], rest[224 * f : 224 * f + 96]], 0)
+        lower = rest[224 * f + 96 : 224 * f + 224]
+        for h, rows in ((0, upper), (1, lower)):
+            put(h, 0, f, rows[:, :128].T)
+            put(h, 1, f, rows[:, 128:].T)
     lanes = sum(bulk[:, 128 * a : 128 * a + 128] for a in range(16))
     return lanes
 
@@ -167,9 +168,25 @@
     return numerator * inverse, time_step * wave_sq * inverse
 
 
-def middle(get, section_at, lane_at, gather, lanes, spread_table, twist, put):
+def all_rates(section_at, lane_at, put):
     lane = lax.broadcasted_iota(jnp.int32, (128, 128), 1)
     row = lax.broadcasted_iota(jnp.int32, (128, 128), 0)
+    slot = 4 * section_at + lane // 32
+    y_index = jnp.where(slot == 0, 8 * lane_at, slot + 16 * lane_at)
+    x_index = row + 128 * (lane % 16)
+    wave_x = wave_square(x_index, NX)
+    wave_xy = wave_x + wave_square(y_index, NY)
+    half_y = (2.0 * math.pi / NY * (NY // 2)) ** 2
+    for sigma in (0, 1):
+        wave_z = wave_square(sigma + 2 * (lane // 16 % 2), NZ)
+        for side, wave_sq in ((0, wave_z + wave_xy), (1, wave_z + (wave_x + half_y))):
+            keep, mix = rates(wave_sq)
+            put(sigma, side, 0, keep)
+            put(sigma, side, 1, mix)
+
+
+def middle(get, get_rate, section_at, lane_at, gather, lanes, spread_table, twist, put):
+    lane = lax.broadcasted_iota(jnp.int32, (128, 128), 1)
     packed = (lane < 32) & (section_at == 0) & (lane_at == 0)
     cos, sin = twist[0], twist[1]
     parts = []
@@ -185,25 +202,21 @@
                 [jnp.concatenate([mixed[0], mixed[2]], 1), jnp.concatenate([mixed[1], mixed[3]], 1)], 0
             )
         )
-    slot = 4 * section_at + lane // 32
-    y_index = jnp.where(slot == 0, 8 * lane_at, slot + 16 * lane_at)
-    x_index = row + 128 * (lane % 16)
-    wave_x = wave_square(x_index, NX)
-    wave_xy = wave_x + wave_square(y_index, NY)
-    half_y = (2.0 * math.pi / NY * (NY // 2)) ** 2
-    back = []
-    for sigma in (0, 1):
-        spread = product(gather, split(stacked[sigma]), NN)
+    spreads = [product(gather, split(stacked[sigma]), NN) for sigma in (0, 1)]
+    turned = []
+    for spread in spreads:
         rows = []
         for f in (0, 1):
             re, im = spread[:128, 128 * f : 128 * f + 128], spread[128:, 128 * f : 128 * f + 128]
             rows.append(jnp.concatenate([re * cos + im * sin, im * cos - re * sin], 1))
-        table = (lanes[sigma, 0], lanes[sigma, 1])
-        spec = product(split(jnp.concatenate(rows, 0)), table, NN)
+        turned.append(split(jnp.concatenate(rows, 0)))
+    tables = [(lanes[sigma, 0], lanes[sigma, 1]) for sigma in (0, 1)]
+    specs = [product(turned[sigma], tables[sigma], NN) for sigma in (0, 1)]
+    filtered = []
+    for sigma, spec in enumerate(specs):
         c_re, c_im, g_re, g_im = spec[:128, :128], spec[:128, 128:], spec[128:, :128], spec[128:, 128:]
-        wave_z = wave_square(sigma + 2 * (lane // 16 % 2), NZ)
-        keep, mix = rates(wave_z + wave_xy)
-        keep_half, mix_half = rates(wave_z + (wave_x + half_y))
+        keep, mix = get_rate(sigma, 0, 0), get_rate(sigma, 0, 1)
+        keep_half, mix_half = get_rate(sigma, 1, 0), get_rate(sigma, 1, 1)
         main_re = keep * c_re - mix * jnp.where(packed, c_im, g_re)
         main_im = keep * c_im - mix * jnp.where(packed, -c_re, g_im)
         side_re = keep_half * g_re - mix_half * g_im
@@ -211,7 +224,8 @@
         rows = jnp.concatenate(
             [jnp.concatenate([main_re, main_im], 1), jnp.concatenate([side_re, side_im], 1)], 0
         )
-        back.append(product(split(rows), table, NT))
+        filtered.append(split(rows))
+    back = [product(filtered[sigma], tables[sigma], NT) for sigma in (0, 1)]
     for s in (0, 1):
         mixed = back[0] + back[1] if s == 0 else back[0] - back[1]
         both = []
@@ -265,8 +279,28 @@
         put(a + 8, even[a] - odd[a])
 
 
+def lane_position():
+    return (
+        16 * lax.axis_index("slab_z")
+        + 4 * lax.axis_index("slab_y")
+        + 2 * lax.axis_index("slab_x")
+        + lax.axis_index("slab_core")
+    )
+
+
 def forward_kernel(
-    c_hbm, fourier_hbm, real_hbm, twist_hbm, out_ref, bulk_ref, c_ref, fourier_ref, real_ref, twist_ref, sems
+    c_hbm,
+    fourier_hbm,
+    real_hbm,
+    twist_hbm,
+    out_ref,
+    bulk_ref,
+    rate_ref,
+    c_ref,
+    fourier_ref,
+    real_ref,
+    twist_ref,
+    sems,
 ):
     sources = (c_hbm, twist_hbm, real_hbm, fourier_hbm)
     targets = (c_ref, twist_ref, real_ref, fourier_ref)
@@ -280,6 +314,9 @@
     def put(h, part, f, value):
         out_ref[pl.ds(512 * h + 2 * part + f, 128, stride=4), :] = value
 
+    def put_rate(sigma, side, kind, value):
+        rate_ref[4 * sigma + 2 * side + kind] = value
+
     def late(n, ref):
         def read():
             copies[n].wait()
@@ -287,13 +324,14 @@
 
         return read
 
+    all_rates(lax.axis_index("section"), lane_position(), put_rate)
     copies[0].wait()
     field = jnp.concatenate([c_ref[0], c_ref[1]], 0)
     lanes = forward_y(field, late(3, fourier_ref), late(2, real_ref), late(1, twist_ref), put)
     bulk_ref[...] = jnp.broadcast_to(jnp.sum(lanes, 0, keepdims=True), (8, 128))
 
 
-def middle_kernel(in_ref, bulk_ref, gather_ref, lanes_ref, spread_ref, twist_ref, out_ref):
+def middle_kernel(in_ref, bulk_ref, rate_ref, gather_ref, lanes_ref, spread_ref, twist_ref, out_ref):
     def get(s, part, f):
         return in_ref[pl.ds(512 * s + 2 * part + f, 128, stride=4), :]
 
@@ -302,11 +340,9 @@
 
     middle(
         get,
+        lambda sigma, side, kind: rate_ref[4 * sigma + 2 * side + kind],
         lax.axis_index("section"),
-        16 * lax.axis_index("slab_z")
-        + 4 * lax.axis_index("slab_y")
-        + 2 * lax.axis_index("slab_x")
-        + lax.axis_index("slab_core"),
+        lane_position(),
         (gather_ref[0], gather_ref[1]),
         lanes_ref,
         (spread_ref[0], spread_ref[1]),
@@ -339,11 +375,15 @@
 def per_device(concentration):
     whole = pl.BlockSpec(memory_space=pltpu.VMEM)
     params = pltpu.CompilerParams(vmem_limit_bytes=12 << 20)
-    outgoing, bulk = pl.pallas_call(
+    outgoing, bulk, rate = pl.pallas_call(
         forward_kernel,
-        out_shape=(pltpu.VMEM((1024, 128), f32), pltpu.VMEM((8, 128), f32)),
+        out_shape=(
+            pltpu.VMEM((1024, 128), f32),
+            pltpu.VMEM((8, 128), f32),
+            pltpu.VMEM((8, 128, 128), f32),
+        ),
         in_specs=[pl.BlockSpec(memory_space=pltpu.HBM)] * 4,
-        out_specs=(whole, whole),
+        out_specs=(whole, whole, whole),
         scratch_shapes=[
             pltpu.VMEM(concentration.shape, f32),
             pltpu.VMEM(FOURIER.shape, bf16),
@@ -352,15 +392,15 @@
             pltpu.SemaphoreType.DMA((4,)),
         ],
         compiler_params=params,
-    )(*[pltpu.with_memory_space_constraint(a, pltpu.HBM) for a in (concentration, FOURIER, REAL, Y_TWIST)])
+    )(*[pltpu.with_memory_space_constraint(a, pltpu.HBM) for a in (concentration, FOURIER_T, REAL_T, Y_TWIST)])
     columns = exchange(outgoing)
     leaving = pl.pallas_call(
         middle_kernel,
         out_shape=jax.ShapeDtypeStruct((768, 128), f32),
-        in_specs=[whole] * 6,
+        in_specs=[whole] * 7,
         out_specs=whole,
         compiler_params=params,
-    )(columns, bulk, GATHER, LANES, SPREAD, X_TWIST)
+    )(columns, bulk, rate, GATHER, LANES, SPREAD, X_TWIST)
     rows_back = exchange(leaving)
     new_field, energy = pl.pallas_call(
         inverse_kernel,

time: 66.1 us -> 65.6 us (level)
  no operation moved by 1% of the time
where the time goes in v5:
time: 65.6 us; the launch traced here: 65.4 us
  blocking collectives  60.2 us (92%)
  Pallas kernels  4.5 us (7%)
  between operations  0.72 us (1%)
    all_to_all x2, blocking collectives, exchange(): lax.all_to_all(message, ALL, split_axis=0, concat_axis=0, tiled=True)  60.2 us
    pallas_call x1, Pallas kernels, per_device(): pl.pallas_call(forward_kernel, out_shape=(pltpu.VMEM((1024, 128), f32), p...  1.99 us
    pallas_call x1, Pallas kernels, per_device(): pl.pallas_call(middle_kernel, out_shape=jax.ShapeDtypeStruct((768, 128),...  1.4 us

profile of v5, /device:TPU:1, one launch (start us, length us, event | category | flops | bytes accessed | tf_op | source)
XLA Modules:
  0.0 65.4 jit_solution(4836289580237985387)
XLA Ops:
  0.6 2.0 %shard_map.113 = (f32[1024,128]{1,0:T(8,128)S(1)}, f32[8,128]{1,0:T(8,128)S(1)}, f32[8,128,128]{2,1,0:T(8,128)S(1)}) custom-call(f32[2,16,2048]{2,1,0:T(8,128)} %c_hbm.1, bf16[2,256,256]{2,1,0:T(8,128)(2,1)} %constant.18.clone.fourier_hbm, bf16[2,256,256]{2,1,0:T(8,128)(2,1)} %constant.19.clone.real_hbm, f32[16,128]{1,0:T(8,128)} %constant.20.clone.twist_hbm.twist_ref), custom_call_target="tpu_custom_call" | custom-call | tf_op jit(solution)/shard_map/pallas_call | solution.py:378
  2.6 0.0 copy-start
  2.6 0.0 copy-start.3
  2.6 0.0 copy-start.4
  2.7 0.0 copy-start.5
  2.7 36.3 %all_to_all.10 = f32[256,1,512]{2,1,0:T(1,128)S(1)} all-to-all(f32[256,1,512]{2,1,0:T(1,128)S(1)} %bitcast.8), channel_id=1, replica_groups=mesh['section'=2,'slab_y'=4,'slab_x'=2,'slab_z'=8,'slab_core'=2] {'secti..., dimensions={0} | all-to-all | bytes 1048576 | tf_op jit(solution)/shard_map/all_to_all | solution.py:372
  39.0 0.0 copy-done
  39.0 0.0 copy-done.3
  39.0 0.0 copy-done.4
  39.0 0.0 copy-done.5
  39.0 1.4 %shard_map.114 = f32[768,128]{1,0:T(8,128)S(1)} custom-call(f32[1024,128]{1,0:T(8,128)S(1)} %bitcast.5, f32[8,128]{1,0:T(8,128)S(1)} %get-tuple-element.8.bulk_ref, f32[8,128,128]{2,1,0:T(8,128)S(1)} %get-tuple-element.9.rate_ref, bf16[2,256,256]{2,1,0:T(8,128)(2,1)S(1)} %copy-done.3, bf16[2,2,256,256]{3,2,1,0:T(8,128)(2,1)S(1)} %copy-done, ...), custom_call_target="tpu_custom_call" | custom-call | tf_op jit(solution)/shard_map/pallas_call | solution.py:397
  40.4 0.0 copy-start.1
  40.4 0.0 copy-start.2
  40.4 0.0 copy-start.6
  40.4 23.9 %all_to_all.11 = f32[256,1,384]{2,1,0:T(1,128)S(1)} all-to-all(f32[256,1,384]{2,1,0:T(1,128)S(1)} %bitcast.6), channel_id=1, replica_groups=mesh['section'=2,'slab_y'=4,'slab_x'=2,'slab_z'=8,'slab_core'=2] {'secti..., dimensions={0} | all-to-all | bytes 786432 | tf_op jit(solution)/shard_map/all_to_all | solution.py:372
  64.3 0.0 copy-done.1
  64.3 0.0 copy-done.2
  64.3 0.0 copy-done.6
  64.3 1.1 %shard_map.115 = (f32[2,16,2048]{2,1,0:T(8,128)}, f32[1,1]{1,0:T(1,128)}) custom-call(f32[768,128]{1,0:T(8,128)S(1)} %bitcast.7, bf16[2,256,256]{2,1,0:T(8,128)(2,1)S(1)} %copy-done.2, bf16[2,256,256]{2,1,0:T(8,128)(2,1)S(1)} %copy-done.1, f32[16,128]{1,0:T(8,128)S(1)} %copy-done.6), custom_call_target="tpu_custom_call" | custom-call | tf_op jit(solution)/shard_map/pallas_call | solution.py:405
Async XLA Ops:
  2.6 36.4 %copy-start = (bf16[2,2,256,256]{3,2,1,0:T(8,128)(2,1)S(1)}, bf16[2,2,256,256]{3,2,1,0:T(8,128)(2,1)}, u32[]{:S(2)}) copy-start(bf16[2,2,256,256]{3,2,1,0:T(8,128)(2,1)} %constant.22.clone.lanes_ref) | copy-start | bytes 1572868
  2.6 36.3 %copy-start.3 = (bf16[2,256,256]{2,1,0:T(8,128)(2,1)S(1)}, bf16[2,256,256]{2,1,0:T(8,128)(2,1)}, u32[]{:S(2)}) copy-start(bf16[2,256,256]{2,1,0:T(8,128)(2,1)} %constant.21.clone.gather_ref) | copy-start | bytes 786436
  2.6 36.3 %copy-start.4 = (f32[2,128,128]{2,1,0:T(8,128)S(1)}, f32[2,128,128]{2,1,0:T(8,128)}, u32[]{:S(2)}) copy-start(f32[2,128,128]{2,1,0:T(8,128)} %constant.24.clone.twist_ref) | copy-start | bytes 393220
  2.7 36.3 %copy-start.5 = (bf16[2,128,256]{2,1,0:T(8,128)(2,1)S(1)}, bf16[2,128,256]{2,1,0:T(8,128)(2,1)}, u32[]{:S(2)}) copy-start(bf16[2,128,256]{2,1,0:T(8,128)(2,1)} %constant.23.clone.spread_ref) | copy-start | bytes 393220
  40.4 23.9 %copy-start.1 = (bf16[2,256,256]{2,1,0:T(8,128)(2,1)S(1)}, bf16[2,256,256]{2,1,0:T(8,128)(2,1)}, u32[]{:S(2)}) copy-start(bf16[2,256,256]{2,1,0:T(8,128)(2,1)} %constant.26.clone.real_ref) | copy-start | bytes 786436
  40.4 23.9 %copy-start.2 = (bf16[2,256,256]{2,1,0:T(8,128)(2,1)S(1)}, bf16[2,256,256]{2,1,0:T(8,128)(2,1)}, u32[]{:S(2)}) copy-start(bf16[2,256,256]{2,1,0:T(8,128)(2,1)} %constant.25.clone.fourier_ref) | copy-start | bytes 786436
  40.4 23.9 %copy-start.6 = (f32[16,128]{1,0:T(8,128)S(1)}, f32[16,128]{1,0:T(8,128)}, u32[]{:S(2)}) copy-start(f32[16,128]{1,0:T(8,128)} %constant.20.clone.twist_hbm.twist_ref) | copy-start | bytes 24580

commit v6 on v5

--- a/solution.py
+++ b/solution.py
@@ -97,62 +97,72 @@
     return both[:total] + (both[total:] + rest)
 
 
-def weighted(terms):
-    total = None
-    for weight, value in terms:
-        if abs(weight) < 1e-12:
-            continue
-        if abs(weight - 1.0) < 1e-12:
-            part = value
-        elif abs(weight + 1.0) < 1e-12:
-            part = -value
-        else:
-            part = value * weight
-        total = part if total is None else total + part
-    return total
-
-
-def y_slots(field):
-    at = [field[:, 128 * a : 128 * a + 128] for a in range(16)]
+def y_slots(at):
     add = [at[a] + at[a + 8] for a in range(8)]
     sub = [at[a] - at[a + 8] for a in range(8)]
-    slots = [
-        jnp.concatenate([(add[0] + add[4]) + (add[2] + add[6]), (add[1] + add[5]) + (add[3] + add[7])], 1)
+    both = [add[a] + add[a + 4] for a in range(4)]
+    diff = [add[a] - add[a + 4] for a in range(4)]
+    zero = jnp.concatenate([both[0] + both[2], both[1] + both[3]], 1)
+    near, far = (diff[1] - diff[3]) * COS16[2], (diff[1] + diff[3]) * COS16[2]
+    minus = [None] + [sub[a] - sub[8 - a] for a in (1, 2, 3)]
+    plus = [None] + [sub[a] + sub[8 - a] for a in (1, 2, 3)]
+    middle_re = minus[2] * COS16[2]
+    re_17, re_35 = sub[0] + middle_re, sub[0] - middle_re
+    re_1, re_3 = minus[1] * COS16[1] + minus[3] * COS16[3], minus[1] * COS16[3] - minus[3] * COS16[1]
+    im_1, im_3 = plus[1] * SIN16[1] + plus[3] * SIN16[3], plus[1] * SIN16[3] - plus[3] * SIN16[1]
+    middle_im = plus[2] * SIN16[2]
+    im_17, im_35 = middle_im + sub[4], middle_im - sub[4]
+    return [
+        zero,
+        (re_17 + re_1, im_1 + im_17, -1),
+        (diff[0] + near, diff[2] + far, -1),
+        (re_35 + re_3, im_3 + im_35, -1),
+        (both[0] - both[2], both[3] - both[1], 1),
+        (re_35 - re_3, im_35 - im_3, 1),
+        (diff[0] - near, diff[2] - far, 1),
+        (re_17 - re_1, im_17 - im_1, 1),
     ]
-    real, imag = {}, {}
-    for j in (2, 4, 6):
-        real[j] = weighted([(COS16[j * a % 16], add[a]) for a in range(8)])
-        imag[j] = weighted([(-SIN16[j * a % 16], add[a]) for a in range(8)])
-    minus = [None] + [sub[a] - sub[8 - a] for a in (1, 2, 3)]
-    plus = [None] + [sub[a] + sub[8 - a] for a in (1, 2, 3)] + [sub[4]]
-    for j in (1, 3, 5, 7):
-        real[j] = weighted([(1.0, sub[0])] + [(COS16[j * a % 16], minus[a]) for a in (1, 2, 3)])
-        imag[j] = weighted([(-SIN16[j * a % 16], plus[a]) for a in (1, 2, 3, 4)])
-    return slots + [(real[j], imag[j]) for j in range(1, 8)]
-
-
-def forward_y(field, read_fourier, read_real, read_twist, put):
-    squared = field * field
-    bulk = squared * (0.25 * squared - 0.5)
-    cubic = squared * field - field
-    both = [y_slots(field), y_slots(cubic)]
-    twist = read_twist()
-    for slots in both:
-        for j in range(1, 8):
-            real, imag = slots[j]
-            cos, sin = twist[j : j + 1], twist[8 + j : 9 + j]
-            slots[j] = jnp.concatenate([real * cos + imag * sin, imag * cos - real * sin], 1)
+
+
+def forward_y(read_rows, read_fourier, read_real, read_twist, put):
+    lanes = None
+    pieces = {}
+    for group in range(4):
+        rows = read_rows(group)
+        c_at, g_at = [], []
+        for a in range(16):
+            value = rows[:, 128 * a : 128 * a + 128]
+            squared = value * value
+            bulk = squared * (0.25 * squared - 0.5)
+            lanes = bulk if lanes is None else lanes + bulk
+            c_at.append(value)
+            g_at.append(squared * value - value)
+        if group == 0:
+            twist = read_twist()
+            turns = [(twist[j : j + 1], twist[8 + j : 9 + j], -twist[j : j + 1]) for j in range(8)]
+        for f, at in enumerate((c_at, g_at)):
+            slots = y_slots(at)
+            pieces[f, 0, group] = slots[0]
+            for j in range(1, 8):
+                re, n, sign = slots[j]
+                cos, sin, negative = turns[j]
+                if sign > 0:
+                    turned = [re * cos + n * sin, n * cos - re * sin]
+                else:
+                    turned = [re * cos - n * sin, n * negative - re * sin]
+                pieces[f, j, group] = jnp.concatenate(turned, 1)
     real_rows = read_real()
-    first = product(split(jnp.concatenate([both[0][0], both[1][0]], 0)), real_rows, NN)
+    zeros = jnp.concatenate([pieces[f, 0, group] for f in (0, 1) for group in range(4)], 0)
+    first = product(split(zeros), real_rows, NN)
     fourier = read_fourier()
-    rest = product(split(jnp.concatenate(both[0][1:] + both[1][1:], 0)), fourier, NN)
+    others = [pieces[f, j, group] for f in (0, 1) for j in range(1, 8) for group in range(4)]
+    rest = product(split(jnp.concatenate(others, 0)), fourier, NN)
     for f in (0, 1):
         upper = jnp.concatenate([first[32 * f : 32 * f + 32], rest[224 * f : 224 * f + 96]], 0)
         lower = rest[224 * f + 96 : 224 * f + 224]
         for h, rows in ((0, upper), (1, lower)):
             put(h, 0, f, rows[:, :128].T)
             put(h, 1, f, rows[:, 128:].T)
-    lanes = sum(bulk[:, 128 * a : 128 * a + 128] for a in range(16))
     return lanes
 
 
@@ -262,21 +272,25 @@
         re, im = slots[j - 1][:, :128], slots[j - 1][:, 128:]
         cos, sin = twist[j : j + 1] * scale, twist[8 + j : 9 + j] * scale
         real[j], imag[j] = re * cos - im * sin, im * cos + re * sin
-    even = [
-        weighted(
-            [(COS16[j * a % 16], real[j]) for j in (2, 4, 6)]
-            + [(-SIN16[j * a % 16], imag[j]) for j in (2, 4, 6)]
-        )
-        + base[a % 2]
-        for a in range(8)
-    ]
-    cosine = [weighted([(COS16[j * a % 16], real[j]) for j in (1, 3, 5, 7)]) for a in range(4)]
-    sine = [None] + [weighted([(SIN16[j * a % 16], imag[j]) for j in (1, 3, 5, 7)]) for a in range(1, 5)]
-    odd = [cosine[0]] + [cosine[a] - sine[a] for a in (1, 2, 3)] + [-sine[4]]
-    odd += [-cosine[a] - sine[a] for a in (3, 2, 1)]
-    for a in range(8):
-        put(a, even[a] + odd[a])
-        put(a + 8, even[a] - odd[a])
+    ends, tips = real[2] + real[6], imag[6] - imag[2]
+    near, far = (real[2] - real[6]) * COS16[2], (imag[2] + imag[6]) * COS16[2]
+    part = [ends, near - far, tips, -(near + far)]
+    four = [base[0] + real[4], base[1] - imag[4], base[0] - real[4], base[1] + imag[4]]
+    even = [four[a] + part[a] for a in range(4)] + [four[a] - part[a] for a in range(4)]
+    u, v, w, x = real[1] + real[7], real[3] + real[5], real[1] - real[7], real[3] - real[5]
+    cosine = [u + v, w * COS16[1] + x * COS16[3], (u - v) * COS16[2], w * COS16[3] - x * COS16[1]]
+    u, v, w, x = imag[1] + imag[7], imag[3] + imag[5], imag[1] - imag[7], imag[3] - imag[5]
+    sine = [None, u * SIN16[1] + v * SIN16[3], (w + x) * SIN16[2], u * SIN16[3] - v * SIN16[1], w - x]
+    put(0, even[0] + cosine[0])
+    put(8, even[0] - cosine[0])
+    for a in (1, 2, 3):
+        odd, mirror = cosine[a] - sine[a], cosine[a] + sine[a]
+        put(a, even[a] + odd)
+        put(a + 8, even[a] - odd)
+        put(8 - a, even[8 - a] - mirror)
+        put(16 - a, even[8 - a] + mirror)
+    put(4, even[4] - sine[4])
+    put(12, even[4] + sine[4])
 
 
 def lane_position():
@@ -302,8 +316,11 @@
     twist_ref,
     sems,
 ):
-    sources = (c_hbm, twist_hbm, real_hbm, fourier_hbm)
-    targets = (c_ref, twist_ref, real_ref, fourier_ref)
+    def group_of(ref, n):
+        return ref.at[n // 2, pl.ds(8 * (n % 2), 8), :]
+
+    sources = [group_of(c_hbm, n) for n in range(4)] + [twist_hbm, real_hbm, fourier_hbm]
+    targets = [group_of(c_ref, n) for n in range(4)] + [twist_ref, real_ref, fourier_ref]
     copies = [
         pltpu.make_async_copy(source, target, sems.at[n])
         for n, (source, target) in enumerate(zip(sources, targets))
@@ -325,9 +342,11 @@
         return read
 
     all_rates(lax.axis_index("section"), lane_position(), put_rate)
-    copies[0].wait()
-    field = jnp.concatenate([c_ref[0], c_ref[1]], 0)
-    lanes = forward_y(field, late(3, fourier_ref), late(2, real_ref), late(1, twist_ref), put)
+    def read_rows(n):
+        copies[n].wait()
+        return c_ref[n // 2, 8 * (n % 2) : 8 * (n % 2) + 8, :]
+
+    lanes = forward_y(read_rows, late(6, fourier_ref), late(5, real_ref), late(4, twist_ref), put)
     bulk_ref[...] = jnp.broadcast_to(jnp.sum(lanes, 0, keepdims=True), (8, 128))
 
 
@@ -389,7 +408,7 @@
             pltpu.VMEM(FOURIER.shape, bf16),
             pltpu.VMEM(REAL.shape, bf16),
             pltpu.VMEM(Y_TWIST.shape, f32),
-            pltpu.SemaphoreType.DMA((4,)),
+            pltpu.SemaphoreType.DMA((7,)),
         ],
         compiler_params=params,
     )(*[pltpu.with_memory_space_constraint(a, pltpu.HBM) for a in (concentration, FOURIER_T, REAL_T, Y_TWIST)])

time: 65.6 us -> 65.4 us (level)
  no operation moved by 1% of the time
where the time goes in v6:
time: 65.4 us; the launch traced here: 65.3 us
  blocking collectives  60.2 us (92%)
  Pallas kernels  4.35 us (7%)
  between operations  0.72 us (1%)
    all_to_all x2, blocking collectives, exchange(): lax.all_to_all(message, ALL, split_axis=0, concat_axis=0, tiled=True)  60.2 us
    pallas_call x1, Pallas kernels, per_device(): pl.pallas_call(forward_kernel, out_shape=(pltpu.VMEM((1024, 128), f32), p...  1.87 us
    pallas_call x1, Pallas kernels, per_device(): pl.pallas_call(middle_kernel, out_shape=jax.ShapeDtypeStruct((768, 128),...  1.4 us

profile of v6, /device:TPU:1, one launch (start us, length us, event | category | flops | bytes accessed | tf_op | source)
XLA Modules:
  0.0 65.3 jit_solution(9991898357745374304)
XLA Ops:
  0.6 1.9 %shard_map.113 = (f32[1024,128]{1,0:T(8,128)S(1)}, f32[8,128]{1,0:T(8,128)S(1)}, f32[8,128,128]{2,1,0:T(8,128)S(1)}) custom-call(f32[2,16,2048]{2,1,0:T(8,128)} %c_hbm.1, bf16[2,256,256]{2,1,0:T(8,128)(2,1)} %constant.18.clone.fourier_hbm, bf16[2,256,256]{2,1,0:T(8,128)(2,1)} %constant.19.clone.real_hbm, f32[16,128]{1,0:T(8,128)} %constant.20.clone.twist_hbm.twist_ref), custom_call_target="tpu_custom_call" | custom-call | tf_op jit(solution)/shard_map/pallas_call | solution.py:397
  2.5 0.0 copy-start
  2.5 0.0 copy-start.3
  2.5 0.0 copy-start.4
  2.5 0.0 copy-start.5
  2.6 36.3 %all_to_all.10 = f32[256,1,512]{2,1,0:T(1,128)S(1)} all-to-all(f32[256,1,512]{2,1,0:T(1,128)S(1)} %bitcast.8), channel_id=1, replica_groups=mesh['section'=2,'slab_y'=4,'slab_x'=2,'slab_z'=8,'slab_core'=2] {'secti..., dimensions={0} | all-to-all | bytes 1048576 | tf_op jit(solution)/shard_map/all_to_all | solution.py:391
  38.9 0.0 copy-done
  38.9 0.0 copy-done.3
  38.9 0.0 copy-done.4
  38.9 0.0 copy-done.5
  38.9 1.4 %shard_map.114 = f32[768,128]{1,0:T(8,128)S(1)} custom-call(f32[1024,128]{1,0:T(8,128)S(1)} %bitcast.5, f32[8,128]{1,0:T(8,128)S(1)} %get-tuple-element.8.bulk_ref, f32[8,128,128]{2,1,0:T(8,128)S(1)} %get-tuple-element.9.rate_ref, bf16[2,256,256]{2,1,0:T(8,128)(2,1)S(1)} %copy-done.3, bf16[2,2,256,256]{3,2,1,0:T(8,128)(2,1)S(1)} %copy-done, ...), custom_call_target="tpu_custom_call" | custom-call | tf_op jit(solution)/shard_map/pallas_call | solution.py:416
  40.3 0.0 copy-start.1
  40.3 0.0 copy-start.2
  40.3 0.0 copy-start.6
  40.3 23.9 %all_to_all.11 = f32[256,1,384]{2,1,0:T(1,128)S(1)} all-to-all(f32[256,1,384]{2,1,0:T(1,128)S(1)} %bitcast.6), channel_id=1, replica_groups=mesh['section'=2,'slab_y'=4,'slab_x'=2,'slab_z'=8,'slab_core'=2] {'secti..., dimensions={0} | all-to-all | bytes 786432 | tf_op jit(solution)/shard_map/all_to_all | solution.py:391
  64.2 0.0 copy-done.1
  64.2 0.0 copy-done.2
  64.2 0.0 copy-done.6
  64.2 1.1 %shard_map.115 = (f32[2,16,2048]{2,1,0:T(8,128)}, f32[1,1]{1,0:T(1,128)}) custom-call(f32[768,128]{1,0:T(8,128)S(1)} %bitcast.7, bf16[2,256,256]{2,1,0:T(8,128)(2,1)S(1)} %copy-done.2, bf16[2,256,256]{2,1,0:T(8,128)(2,1)S(1)} %copy-done.1, f32[16,128]{1,0:T(8,128)S(1)} %copy-done.6), custom_call_target="tpu_custom_call" | custom-call | tf_op jit(solution)/shard_map/pallas_call | solution.py:424
Async XLA Ops:
  2.5 36.4 %copy-start = (bf16[2,2,256,256]{3,2,1,0:T(8,128)(2,1)S(1)}, bf16[2,2,256,256]{3,2,1,0:T(8,128)(2,1)}, u32[]{:S(2)}) copy-start(bf16[2,2,256,256]{3,2,1,0:T(8,128)(2,1)} %constant.22.clone.lanes_ref) | copy-start | bytes 1572868
  2.5 36.3 %copy-start.3 = (bf16[2,256,256]{2,1,0:T(8,128)(2,1)S(1)}, bf16[2,256,256]{2,1,0:T(8,128)(2,1)}, u32[]{:S(2)}) copy-start(bf16[2,256,256]{2,1,0:T(8,128)(2,1)} %constant.21.clone.gather_ref) | copy-start | bytes 786436
  2.5 36.3 %copy-start.4 = (f32[2,128,128]{2,1,0:T(8,128)S(1)}, f32[2,128,128]{2,1,0:T(8,128)}, u32[]{:S(2)}) copy-start(f32[2,128,128]{2,1,0:T(8,128)} %constant.24.clone.twist_ref) | copy-start | bytes 393220
  2.5 36.3 %copy-start.5 = (bf16[2,128,256]{2,1,0:T(8,128)(2,1)S(1)}, bf16[2,128,256]{2,1,0:T(8,128)(2,1)}, u32[]{:S(2)}) copy-start(bf16[2,128,256]{2,1,0:T(8,128)(2,1)} %constant.23.clone.spread_ref) | copy-start | bytes 393220
  40.3 23.9 %copy-start.1 = (bf16[2,256,256]{2,1,0:T(8,128)(2,1)S(1)}, bf16[2,256,256]{2,1,0:T(8,128)(2,1)}, u32[]{:S(2)}) copy-start(bf16[2,256,256]{2,1,0:T(8,128)(2,1)} %constant.26.clone.real_ref) | copy-start | bytes 786436
  40.3 23.9 %copy-start.2 = (bf16[2,256,256]{2,1,0:T(8,128)(2,1)S(1)}, bf16[2,256,256]{2,1,0:T(8,128)(2,1)}, u32[]{:S(2)}) copy-start(bf16[2,256,256]{2,1,0:T(8,128)(2,1)} %constant.25.clone.fourier_ref) | copy-start | bytes 786436
  40.3 23.9 %copy-start.6 = (f32[16,128]{1,0:T(8,128)S(1)}, f32[16,128]{1,0:T(8,128)}, u32[]{:S(2)}) copy-start(f32[16,128]{1,0:T(8,128)} %constant.20.clone.twist_hbm.twist_ref) | copy-start | bytes 24580

commit v7 on v6

--- a/solution.py
+++ b/solution.py
@@ -308,7 +308,6 @@
     real_hbm,
     twist_hbm,
     out_ref,
-    bulk_ref,
     rate_ref,
     c_ref,
     fourier_ref,
@@ -329,7 +328,7 @@
         copy.start()
 
     def put(h, part, f, value):
-        out_ref[pl.ds(512 * h + 2 * part + f, 128, stride=4), :] = value
+        out_ref[pl.ds(640 * h + 2 * part + f, 128, stride=5), :] = value
 
     def put_rate(sigma, side, kind, value):
         rate_ref[4 * sigma + 2 * side + kind] = value
@@ -347,15 +346,17 @@
         return c_ref[n // 2, 8 * (n % 2) : 8 * (n % 2) + 8, :]
 
     lanes = forward_y(read_rows, late(6, fourier_ref), late(5, real_ref), late(4, twist_ref), put)
-    bulk_ref[...] = jnp.broadcast_to(jnp.sum(lanes, 0, keepdims=True), (8, 128))
-
-
-def middle_kernel(in_ref, bulk_ref, rate_ref, gather_ref, lanes_ref, spread_ref, twist_ref, out_ref):
+    out_ref[pl.ds(4, 256, stride=5), :] = jnp.broadcast_to(jnp.sum(lanes, 0, keepdims=True), (256, 128))
+
+
+def middle_kernel(
+    in_ref, rate_ref, gather_ref, lanes_ref, spread_ref, twist_ref, out_ref, bulk_ref
+):
     def get(s, part, f):
-        return in_ref[pl.ds(512 * s + 2 * part + f, 128, stride=4), :]
+        return in_ref[pl.ds(640 * s + 2 * part + f, 128, stride=5), :]
 
     def put(s, part, value):
-        out_ref[pl.ds(384 * s + part, 128, stride=3), :] = value
+        out_ref[pl.ds(256 * s + part, 128, stride=2), :] = value
 
     middle(
         get,
@@ -368,21 +369,22 @@
         twist_ref,
         put,
     )
-    out_ref[pl.ds(2, 256, stride=3), :] = jnp.broadcast_to(bulk_ref[0:1, :], (256, 128))
-
-
-def inverse_kernel(in_ref, fourier_ref, real_ref, twist_ref, out_ref, energy_ref):
+    bulk = jnp.sum(in_ref[pl.ds(4, 256, stride=5), :], 0, keepdims=True)
+    bulk_ref[...] = jnp.broadcast_to(bulk, (8, 128))
+
+
+def inverse_kernel(in_ref, bulk_ref, fourier_ref, real_ref, twist_ref, out_ref, energy_ref):
     def get(h, part):
-        return in_ref[pl.ds(384 * h + part, 128, stride=3), :]
+        return in_ref[pl.ds(256 * h + part, 128, stride=2), :]
 
     def put(a, value):
         out_ref[0, :, 128 * a : 128 * a + 128] = value[:16]
         out_ref[1, :, 128 * a : 128 * a + 128] = value[16:]
 
+    energy_ref[...] = jnp.sum(bulk_ref[0:1, :], keepdims=True) * (1.0 / CELLS)
     inverse_y(
         get, (fourier_ref[0], fourier_ref[1]), (real_ref[0], real_ref[1]), twist_ref[...], put
     )
-    energy_ref[...] = jnp.sum(in_ref[pl.ds(2, 256, stride=3), :], keepdims=True) * (1.0 / CELLS)
 
 
 def exchange(rows):
@@ -394,15 +396,14 @@
 def per_device(concentration):
     whole = pl.BlockSpec(memory_space=pltpu.VMEM)
     params = pltpu.CompilerParams(vmem_limit_bytes=12 << 20)
-    outgoing, bulk, rate = pl.pallas_call(
+    outgoing, rate = pl.pallas_call(
         forward_kernel,
         out_shape=(
-            pltpu.VMEM((1024, 128), f32),
-            pltpu.VMEM((8, 128), f32),
+            pltpu.VMEM((1280, 128), f32),
             pltpu.VMEM((8, 128, 128), f32),
         ),
         in_specs=[pl.BlockSpec(memory_space=pltpu.HBM)] * 4,
-        out_specs=(whole, whole, whole),
+        out_specs=(whole, whole),
         scratch_shapes=[
             pltpu.VMEM(concentration.shape, f32),
             pltpu.VMEM(FOURIER.shape, bf16),
@@ -413,21 +414,21 @@
         compiler_params=params,
     )(*[pltpu.with_memory_space_constraint(a, pltpu.HBM) for a in (concentration, FOURIER_T, REAL_T, Y_TWIST)])
     columns = exchange(outgoing)
-    leaving = pl.pallas_call(
+    leaving, bulk = pl.pallas_call(
         middle_kernel,
-        out_shape=jax.ShapeDtypeStruct((768, 128), f32),
-        in_specs=[whole] * 7,
-        out_specs=whole,
+        out_shape=(pltpu.VMEM((512, 128), f32), pltpu.VMEM((8, 128), f32)),
+        in_specs=[whole] * 6,
+        out_specs=(whole, whole),
         compiler_params=params,
-    )(columns, bulk, rate, GATHER, LANES, SPREAD, X_TWIST)
+    )(columns, rate, GATHER, LANES, SPREAD, X_TWIST)
     rows_back = exchange(leaving)
     new_field, energy = pl.pallas_call(
         inverse_kernel,
         out_shape=(jax.ShapeDtypeStruct(concentration.shape, f32), jax.ShapeDtypeStruct((1, 1), f32)),
-        in_specs=[whole] * 4,
+        in_specs=[whole] * 5,
         out_specs=(whole, whole),
         compiler_params=params,
-    )(rows_back, FOURIER, REAL, Y_TWIST)
+    )(rows_back, bulk, FOURIER, REAL, Y_TWIST)
     return new_field, energy.reshape(())
 
 

time: 65.4 us -> 65.3 us (level)
  no operation moved by 1% of the time
where the time goes in v7:
time: 65.3 us; the launch traced here: 65.2 us
  blocking collectives  60.1 us (92%)
  Pallas kernels  4.33 us (7%)
  between operations  0.72 us (1%)
    all_to_all x2, blocking collectives, exchange(): lax.all_to_all(message, ALL, split_axis=0, concat_axis=0, tiled=True)  60.1 us
    pallas_call x1, Pallas kernels, per_device(): pl.pallas_call(forward_kernel, out_shape=(pltpu.VMEM((1280, 128), f32), p...  1.87 us
    pallas_call x1, Pallas kernels, per_device(): pl.pallas_call(middle_kernel, out_shape=(pltpu.VMEM((512, 128), f32), plt...  1.38 us

profile of v7, /device:TPU:1, one launch (start us, length us, event | category | flops | bytes accessed | tf_op | source)
XLA Modules:
  0.0 65.2 jit_solution(12631640173882949202)
XLA Ops:
  0.6 1.9 %shard_map.113 = (f32[1280,128]{1,0:T(8,128)S(1)}, f32[8,128,128]{2,1,0:T(8,128)S(1)}) custom-call(f32[2,16,2048]{2,1,0:T(8,128)} %c_hbm.1, bf16[2,256,256]{2,1,0:T(8,128)(2,1)} %constant.18.clone.fourier_hbm, bf16[2,256,256]{2,1,0:T(8,128)(2,1)} %constant.19.clone.real_hbm, f32[16,128]{1,0:T(8,128)} %constant.20.clone.twist_hbm.twist_ref), custom_call_target="tpu_custom_call" | custom-call | tf_op jit(solution)/shard_map/pallas_call | solution.py:399
  2.5 0.0 copy-start
  2.5 0.0 copy-start.3
  2.5 0.0 copy-start.4
  2.5 0.0 copy-start.5
  2.6 38.6 %all_to_all.10 = f32[256,1,640]{2,1,0:T(1,128)S(1)} all-to-all(f32[256,1,640]{2,1,0:T(1,128)S(1)} %bitcast.7), channel_id=1, replica_groups=mesh['section'=2,'slab_y'=4,'slab_x'=2,'slab_z'=8,'slab_core'=2] {'secti..., dimensions={0} | all-to-all | bytes 1310720 | tf_op jit(solution)/shard_map/all_to_all | solution.py:393
  41.1 0.0 copy-done
  41.1 0.0 copy-done.3
  41.1 0.0 copy-done.4
  41.1 0.0 copy-done.5
  41.2 0.0 copy-start.6
  41.2 1.4 %shard_map.114 = (f32[512,128]{1,0:T(8,128)S(1)}, f32[8,128]{1,0:T(8,128)S(1)}) custom-call(f32[1280,128]{1,0:T(8,128)S(1)} %bitcast.5, f32[8,128,128]{2,1,0:T(8,128)S(1)} %get-tuple-element.9.rate_ref, bf16[2,256,256]{2,1,0:T(8,128)(2,1)S(1)} %copy-done.3, bf16[2,2,256,256]{3,2,1,0:T(8,128)(2,1)S(1)} %copy-done, bf16[2,128,256]{2,1,0:T(8,128)(2,1)S(1)} %copy-done.5, ...), custom_call_target="tpu_custom_call" | custom-call | tf_op jit(solution)/shard_map/pallas_call | solution.py:417
  42.6 0.0 copy-start.1
  42.6 0.0 copy-start.2
  42.6 21.5 %all_to_all.11 = f32[256,1,256]{2,1,0:T(1,128)S(1)} all-to-all(f32[256,1,256]{2,1,0:T(1,128)S(1)} %bitcast.8), channel_id=1, replica_groups=mesh['section'=2,'slab_y'=4,'slab_x'=2,'slab_z'=8,'slab_core'=2] {'secti..., dimensions={0} | all-to-all | bytes 524288 | tf_op jit(solution)/shard_map/all_to_all | solution.py:393
  64.1 0.0 copy-done.6
  64.1 0.0 copy-done.1
  64.1 0.0 copy-done.2
  64.1 1.1 %shard_map.115 = (f32[2,16,2048]{2,1,0:T(8,128)}, f32[1,1]{1,0:T(1,128)}) custom-call(f32[512,128]{1,0:T(8,128)S(1)} %bitcast.6, f32[8,128]{1,0:T(8,128)S(1)} %get-tuple-element.11.bulk_ref, bf16[2,256,256]{2,1,0:T(8,128)(2,1)S(1)} %copy-done.2, bf16[2,256,256]{2,1,0:T(8,128)(2,1)S(1)} %copy-done.1, f32[16,128]{1,0:T(8,128)S(1)} %copy-done.6), custom_call_target="tpu_custom_call" | custom-call | tf_op jit(solution)/shard_map/pallas_call | solution.py:425
Async XLA Ops:
  2.5 38.6 %copy-start = (bf16[2,2,256,256]{3,2,1,0:T(8,128)(2,1)S(1)}, bf16[2,2,256,256]{3,2,1,0:T(8,128)(2,1)}, u32[]{:S(2)}) copy-start(bf16[2,2,256,256]{3,2,1,0:T(8,128)(2,1)} %constant.22.clone.lanes_ref) | copy-start | bytes 1572868
  2.5 38.6 %copy-start.3 = (bf16[2,256,256]{2,1,0:T(8,128)(2,1)S(1)}, bf16[2,256,256]{2,1,0:T(8,128)(2,1)}, u32[]{:S(2)}) copy-start(bf16[2,256,256]{2,1,0:T(8,128)(2,1)} %constant.21.clone.gather_ref) | copy-start | bytes 786436
  2.5 38.6 %copy-start.4 = (f32[2,128,128]{2,1,0:T(8,128)S(1)}, f32[2,128,128]{2,1,0:T(8,128)}, u32[]{:S(2)}) copy-start(f32[2,128,128]{2,1,0:T(8,128)} %constant.24.clone.twist_ref) | copy-start | bytes 393220
  2.5 38.6 %copy-start.5 = (bf16[2,128,256]{2,1,0:T(8,128)(2,1)S(1)}, bf16[2,128,256]{2,1,0:T(8,128)(2,1)}, u32[]{:S(2)}) copy-start(bf16[2,128,256]{2,1,0:T(8,128)(2,1)} %constant.23.clone.spread_ref) | copy-start | bytes 393220
  41.2 22.9 %copy-start.6 = (f32[16,128]{1,0:T(8,128)S(1)}, f32[16,128]{1,0:T(8,128)}, u32[]{:S(2)}) copy-start(f32[16,128]{1,0:T(8,128)} %constant.20.clone.twist_hbm.twist_ref) | copy-start | bytes 24580
  42.6 21.5 %copy-start.1 = (bf16[2,256,256]{2,1,0:T(8,128)(2,1)S(1)}, bf16[2,256,256]{2,1,0:T(8,128)(2,1)}, u32[]{:S(2)}) copy-start(bf16[2,256,256]{2,1,0:T(8,128)(2,1)} %constant.26.clone.real_ref) | copy-start | bytes 786436
  42.6 21.5 %copy-start.2 = (bf16[2,256,256]{2,1,0:T(8,128)(2,1)S(1)}, bf16[2,256,256]{2,1,0:T(8,128)(2,1)}, u32[]{:S(2)}) copy-start(bf16[2,256,256]{2,1,0:T(8,128)(2,1)} %constant.25.clone.fourier_ref) | copy-start | bytes 786436

commit v8 on v7

--- a/solution.py
+++ b/solution.py
@@ -124,43 +124,45 @@
     ]
 
 
+def turned_slots(at, turns):
+    slots = y_slots(at)
+    for j in range(1, 8):
+        re, n, sign = slots[j]
+        cos, sin, negative = turns[j]
+        if sign > 0:
+            turned = [re * cos + n * sin, n * cos - re * sin]
+        else:
+            turned = [re * cos - n * sin, n * negative - re * sin]
+        slots[j] = jnp.concatenate(turned, 1)
+    return slots
+
+
 def forward_y(read_rows, read_fourier, read_real, read_twist, put):
-    lanes = None
-    pieces = {}
+    twist = read_twist()
+    turns = [(twist[j : j + 1], twist[8 + j : 9 + j], -twist[j : j + 1]) for j in range(8)]
+    blocks, slots = [], []
     for group in range(4):
         rows = read_rows(group)
-        c_at, g_at = [], []
-        for a in range(16):
-            value = rows[:, 128 * a : 128 * a + 128]
-            squared = value * value
-            bulk = squared * (0.25 * squared - 0.5)
-            lanes = bulk if lanes is None else lanes + bulk
-            c_at.append(value)
-            g_at.append(squared * value - value)
-        if group == 0:
-            twist = read_twist()
-            turns = [(twist[j : j + 1], twist[8 + j : 9 + j], -twist[j : j + 1]) for j in range(8)]
-        for f, at in enumerate((c_at, g_at)):
-            slots = y_slots(at)
-            pieces[f, 0, group] = slots[0]
-            for j in range(1, 8):
-                re, n, sign = slots[j]
-                cos, sin, negative = turns[j]
-                if sign > 0:
-                    turned = [re * cos + n * sin, n * cos - re * sin]
-                else:
-                    turned = [re * cos - n * sin, n * negative - re * sin]
-                pieces[f, j, group] = jnp.concatenate(turned, 1)
+        blocks.append([rows[:, 128 * a : 128 * a + 128] for a in range(16)])
+        slots.append(turned_slots(blocks[group], turns))
     real_rows = read_real()
-    zeros = jnp.concatenate([pieces[f, 0, group] for f in (0, 1) for group in range(4)], 0)
-    first = product(split(zeros), real_rows, NN)
     fourier = read_fourier()
-    others = [pieces[f, j, group] for f in (0, 1) for j in range(1, 8) for group in range(4)]
-    rest = product(split(jnp.concatenate(others, 0)), fourier, NN)
+    lanes = None
     for f in (0, 1):
-        upper = jnp.concatenate([first[32 * f : 32 * f + 32], rest[224 * f : 224 * f + 96]], 0)
-        lower = rest[224 * f + 96 : 224 * f + 224]
-        for h, rows in ((0, upper), (1, lower)):
+        if f == 1:
+            slots = []
+            for block in blocks:
+                cubic = []
+                for value in block:
+                    squared = value * value
+                    bulk = squared * (0.25 * squared - 0.5)
+                    lanes = bulk if lanes is None else lanes + bulk
+                    cubic.append(squared * value - value)
+                slots.append(turned_slots(cubic, turns))
+        first = product(split(jnp.concatenate([slot[0] for slot in slots], 0)), real_rows, NN)
+        others = [slot[j] for j in range(1, 8) for slot in slots]
+        rest = product(split(jnp.concatenate(others, 0)), fourier, NN)
+        for h, rows in ((0, jnp.concatenate([first, rest[:96]], 0)), (1, rest[96:])):
             put(h, 0, f, rows[:, :128].T)
             put(h, 1, f, rows[:, 128:].T)
     return lanes
@@ -318,8 +320,8 @@
     def group_of(ref, n):
         return ref.at[n // 2, pl.ds(8 * (n % 2), 8), :]
 
-    sources = [group_of(c_hbm, n) for n in range(4)] + [twist_hbm, real_hbm, fourier_hbm]
-    targets = [group_of(c_ref, n) for n in range(4)] + [twist_ref, real_ref, fourier_ref]
+    sources = [twist_hbm] + [group_of(c_hbm, n) for n in range(4)] + [real_hbm, fourier_hbm]
+    targets = [twist_ref] + [group_of(c_ref, n) for n in range(4)] + [real_ref, fourier_ref]
     copies = [
         pltpu.make_async_copy(source, target, sems.at[n])
         for n, (source, target) in enumerate(zip(sources, targets))
@@ -342,10 +344,10 @@
 
     all_rates(lax.axis_index("section"), lane_position(), put_rate)
     def read_rows(n):
-        copies[n].wait()
+        copies[n + 1].wait()
         return c_ref[n // 2, 8 * (n % 2) : 8 * (n % 2) + 8, :]
 
-    lanes = forward_y(read_rows, late(6, fourier_ref), late(5, real_ref), late(4, twist_ref), put)
+    lanes = forward_y(read_rows, late(6, fourier_ref), late(5, real_ref), late(0, twist_ref), put)
     out_ref[pl.ds(4, 256, stride=5), :] = jnp.broadcast_to(jnp.sum(lanes, 0, keepdims=True), (256, 128))
 
 

time: 65.3 us -> 65.2 us (level)
  no operation moved by 1% of the time
where the time goes in v8:
time: 65.2 us; the launch traced here: 65 us
  blocking collectives  60.1 us (92%)
  Pallas kernels  4.22 us (6%)
  between operations  0.72 us (1%)
    all_to_all x2, blocking collectives, exchange(): lax.all_to_all(message, ALL, split_axis=0, concat_axis=0, tiled=True)  60.1 us
    pallas_call x1, Pallas kernels, per_device(): pl.pallas_call(forward_kernel, out_shape=(pltpu.VMEM((1280, 128), f32), p...  1.75 us
    pallas_call x1, Pallas kernels, per_device(): pl.pallas_call(middle_kernel, out_shape=(pltpu.VMEM((512, 128), f32), plt...  1.38 us

profile of v8, /device:TPU:1, one launch (start us, length us, event | category | flops | bytes accessed | tf_op | source)
XLA Modules:
  0.0 65.0 jit_solution(12189813507109669298)
XLA Ops:
  0.6 1.8 %shard_map.113 = (f32[1280,128]{1,0:T(8,128)S(1)}, f32[8,128,128]{2,1,0:T(8,128)S(1)}) custom-call(f32[2,16,2048]{2,1,0:T(8,128)} %c_hbm.1, bf16[2,256,256]{2,1,0:T(8,128)(2,1)} %constant.18.clone.fourier_hbm, bf16[2,256,256]{2,1,0:T(8,128)(2,1)} %constant.19.clone.real_hbm, f32[16,128]{1,0:T(8,128)} %constant.20.clone.twist_hbm.twist_ref), custom_call_target="tpu_custom_call" | custom-call | tf_op jit(solution)/shard_map/pallas_call | solution.py:401
  2.4 0.0 copy-start
  2.4 0.0 copy-start.3
  2.4 0.0 copy-start.4
  2.4 0.0 copy-start.5
  2.4 38.6 %all_to_all.10 = f32[256,1,640]{2,1,0:T(1,128)S(1)} all-to-all(f32[256,1,640]{2,1,0:T(1,128)S(1)} %bitcast.7), channel_id=1, replica_groups=mesh['section'=2,'slab_y'=4,'slab_x'=2,'slab_z'=8,'slab_core'=2] {'secti..., dimensions={0} | all-to-all | bytes 1310720 | tf_op jit(solution)/shard_map/all_to_all | solution.py:395
  41.0 0.0 copy-done
  41.0 0.0 copy-done.3
  41.0 0.0 copy-done.4
  41.0 0.0 copy-done.5
  41.0 0.0 copy-start.6
  41.1 1.4 %shard_map.114 = (f32[512,128]{1,0:T(8,128)S(1)}, f32[8,128]{1,0:T(8,128)S(1)}) custom-call(f32[1280,128]{1,0:T(8,128)S(1)} %bitcast.5, f32[8,128,128]{2,1,0:T(8,128)S(1)} %get-tuple-element.9.rate_ref, bf16[2,256,256]{2,1,0:T(8,128)(2,1)S(1)} %copy-done.3, bf16[2,2,256,256]{3,2,1,0:T(8,128)(2,1)S(1)} %copy-done, bf16[2,128,256]{2,1,0:T(8,128)(2,1)S(1)} %copy-done.5, ...), custom_call_target="tpu_custom_call" | custom-call | tf_op jit(solution)/shard_map/pallas_call | solution.py:419
  42.4 0.0 copy-start.1
  42.5 0.0 copy-start.2
  42.5 21.5 %all_to_all.11 = f32[256,1,256]{2,1,0:T(1,128)S(1)} all-to-all(f32[256,1,256]{2,1,0:T(1,128)S(1)} %bitcast.8), channel_id=1, replica_groups=mesh['section'=2,'slab_y'=4,'slab_x'=2,'slab_z'=8,'slab_core'=2] {'secti..., dimensions={0} | all-to-all | bytes 524288 | tf_op jit(solution)/shard_map/all_to_all | solution.py:395
  63.9 0.0 copy-done.6
  64.0 0.0 copy-done.1
  64.0 0.0 copy-done.2
  64.0 1.1 %shard_map.115 = (f32[2,16,2048]{2,1,0:T(8,128)}, f32[1,1]{1,0:T(1,128)}) custom-call(f32[512,128]{1,0:T(8,128)S(1)} %bitcast.6, f32[8,128]{1,0:T(8,128)S(1)} %get-tuple-element.11.bulk_ref, bf16[2,256,256]{2,1,0:T(8,128)(2,1)S(1)} %copy-done.2, bf16[2,256,256]{2,1,0:T(8,128)(2,1)S(1)} %copy-done.1, f32[16,128]{1,0:T(8,128)S(1)} %copy-done.6), custom_call_target="tpu_custom_call" | custom-call | tf_op jit(solution)/shard_map/pallas_call | solution.py:427
Async XLA Ops:
  2.4 38.6 %copy-start = (bf16[2,2,256,256]{3,2,1,0:T(8,128)(2,1)S(1)}, bf16[2,2,256,256]{3,2,1,0:T(8,128)(2,1)}, u32[]{:S(2)}) copy-start(bf16[2,2,256,256]{3,2,1,0:T(8,128)(2,1)} %constant.22.clone.lanes_ref) | copy-start | bytes 1572868
  2.4 38.6 %copy-start.3 = (bf16[2,256,256]{2,1,0:T(8,128)(2,1)S(1)}, bf16[2,256,256]{2,1,0:T(8,128)(2,1)}, u32[]{:S(2)}) copy-start(bf16[2,256,256]{2,1,0:T(8,128)(2,1)} %constant.21.clone.gather_ref) | copy-start | bytes 786436
  2.4 38.6 %copy-start.4 = (f32[2,128,128]{2,1,0:T(8,128)S(1)}, f32[2,128,128]{2,1,0:T(8,128)}, u32[]{:S(2)}) copy-start(f32[2,128,128]{2,1,0:T(8,128)} %constant.24.clone.twist_ref) | copy-start | bytes 393220
  2.4 38.6 %copy-start.5 = (bf16[2,128,256]{2,1,0:T(8,128)(2,1)S(1)}, bf16[2,128,256]{2,1,0:T(8,128)(2,1)}, u32[]{:S(2)}) copy-start(bf16[2,128,256]{2,1,0:T(8,128)(2,1)} %constant.23.clone.spread_ref) | copy-start | bytes 393220
  41.0 22.9 %copy-start.6 = (f32[16,128]{1,0:T(8,128)S(1)}, f32[16,128]{1,0:T(8,128)}, u32[]{:S(2)}) copy-start(f32[16,128]{1,0:T(8,128)} %constant.20.clone.twist_hbm.twist_ref) | copy-start | bytes 24580
  42.4 21.5 %copy-start.1 = (bf16[2,256,256]{2,1,0:T(8,128)(2,1)S(1)}, bf16[2,256,256]{2,1,0:T(8,128)(2,1)}, u32[]{:S(2)}) copy-start(bf16[2,256,256]{2,1,0:T(8,128)(2,1)} %constant.26.clone.real_ref) | copy-start | bytes 786436
  42.5 21.5 %copy-start.2 = (bf16[2,256,256]{2,1,0:T(8,128)(2,1)S(1)}, bf16[2,256,256]{2,1,0:T(8,128)(2,1)}, u32[]{:S(2)}) copy-start(bf16[2,256,256]{2,1,0:T(8,128)(2,1)} %constant.25.clone.fourier_ref) | copy-start | bytes 786436

commit v9 on v8

--- a/solution.py
+++ b/solution.py
@@ -68,7 +68,7 @@
 FOURIER = fourier_table()
 ORDER = slab_order()
 GATHER = FOURIER[:, :, np.concatenate([ORDER, 128 + ORDER])]
-SPREAD = FOURIER[:, ORDER, :]
+SPREAD = np.concatenate([FOURIER[:, ORDER, :128], -FOURIER[:, ORDER, 128:]], 2)
 REAL = real_table()
 LANES = np.stack([lane_table(0), lane_table(1)])
 FOURIER_T = FOURIER.transpose(0, 2, 1)
@@ -189,15 +189,30 @@
     wave_x = wave_square(x_index, NX)
     wave_xy = wave_x + wave_square(y_index, NY)
     half_y = (2.0 * math.pi / NY * (NY // 2)) ** 2
+    side_row = lax.broadcasted_iota(jnp.int32, (32, 128), 0)
+    side_lane = lax.broadcasted_iota(jnp.int32, (32, 128), 1)
+    side_x = wave_square(side_row + 32 * (side_lane // 32) + 128 * (side_lane % 16), NX)
     for sigma in (0, 1):
-        wave_z = wave_square(sigma + 2 * (lane // 16 % 2), NZ)
-        for side, wave_sq in ((0, wave_z + wave_xy), (1, wave_z + (wave_x + half_y))):
-            keep, mix = rates(wave_sq)
-            put(sigma, side, 0, keep)
-            put(sigma, side, 1, mix)
-
-
-def middle(get, get_rate, section_at, lane_at, gather, lanes, spread_table, twist, put):
+        for kind, value in enumerate(rates(wave_square(sigma + 2 * (lane // 16 % 2), NZ) + wave_xy)):
+            put(sigma, 0, kind, value)
+        side_z = wave_square(sigma + 2 * (side_lane // 16 % 2), NZ)
+        for kind, value in enumerate(rates(side_z + (side_x + half_y))):
+            put(sigma, 1, kind, value)
+
+
+def pack(value, roll):
+    lane = lax.broadcasted_iota(jnp.int32, (32, 128), 1)
+    total = value[:32]
+    for n in (1, 2, 3):
+        total = jnp.where(lane // 32 == n, roll(value[32 * n : 32 * n + 32], 32 * n, 1), total)
+    return total
+
+
+def unpack(value, roll):
+    return jnp.concatenate([value] + [roll(value, 128 - 32 * n, 1) for n in (1, 2, 3)], 0)
+
+
+def middle(roll, get, get_rate, section_at, lane_at, gather, lanes, spread_table, twist, put):
     lane = lax.broadcasted_iota(jnp.int32, (128, 128), 1)
     packed = (lane < 32) & (section_at == 0) & (lane_at == 0)
     cos, sin = twist[0], twist[1]
@@ -231,6 +246,7 @@
         keep_half, mix_half = get_rate(sigma, 1, 0), get_rate(sigma, 1, 1)
         main_re = keep * c_re - mix * jnp.where(packed, c_im, g_re)
         main_im = keep * c_im - mix * jnp.where(packed, -c_re, g_im)
+        g_re, g_im = pack(g_re, roll), pack(g_im, roll)
         side_re = keep_half * g_re - mix_half * g_im
         side_im = keep_half * g_im + mix_half * g_re
         rows = jnp.concatenate(
@@ -240,13 +256,11 @@
     back = [product(filtered[sigma], tables[sigma], NT) for sigma in (0, 1)]
     for s in (0, 1):
         mixed = back[0] + back[1] if s == 0 else back[0] - back[1]
-        both = []
-        for f in (0, 1):
-            re, im = mixed[128 * f : 128 * f + 128, :128], mixed[128 * f : 128 * f + 128, 128:]
-            both.append((re * cos - im * sin, im * cos + re * sin))
-        (m_re, m_im), (s_re, s_im) = both
-        upper = jnp.concatenate([m_re, jnp.where(packed, s_re, m_im)], 1)
-        lower = jnp.concatenate([-m_im, jnp.where(packed, -s_im, m_re)], 1)
+        re, im = mixed[:128, :128], mixed[:128, 128:]
+        side_re, side_im = unpack(mixed[128:, :128], roll), unpack(mixed[128:, 128:], roll)
+        other_re, other_im = jnp.where(packed, side_re, im), jnp.where(packed, side_im, -re)
+        upper = jnp.concatenate([re * cos - im * sin, other_re * cos - other_im * sin], 1)
+        lower = jnp.concatenate([im * cos + re * sin, other_im * cos + other_re * sin], 1)
         out = product(spread_table, split(jnp.concatenate([upper, lower], 0)), NN)
         put(s, 0, out[:, :128])
         put(s, 1, out[:, 128:])
@@ -311,6 +325,7 @@
     twist_hbm,
     out_ref,
     rate_ref,
+    side_ref,
     c_ref,
     fourier_ref,
     real_ref,
@@ -333,7 +348,7 @@
         out_ref[pl.ds(640 * h + 2 * part + f, 128, stride=5), :] = value
 
     def put_rate(sigma, side, kind, value):
-        rate_ref[4 * sigma + 2 * side + kind] = value
+        (rate_ref, side_ref)[side][2 * sigma + kind] = value
 
     def late(n, ref):
         def read():
@@ -352,7 +367,7 @@
 
 
 def middle_kernel(
-    in_ref, rate_ref, gather_ref, lanes_ref, spread_ref, twist_ref, out_ref, bulk_ref
+    in_ref, rate_ref, side_ref, gather_ref, lanes_ref, spread_ref, twist_ref, out_ref, bulk_ref
 ):
     def get(s, part, f):
         return in_ref[pl.ds(640 * s + 2 * part + f, 128, stride=5), :]
@@ -361,8 +376,9 @@
         out_ref[pl.ds(256 * s + part, 128, stride=2), :] = value
 
     middle(
+        pltpu.roll,
         get,
-        lambda sigma, side, kind: rate_ref[4 * sigma + 2 * side + kind],
+        lambda sigma, side, kind: (rate_ref, side_ref)[side][2 * sigma + kind],
         lax.axis_index("section"),
         lane_position(),
         (gather_ref[0], gather_ref[1]),
@@ -398,14 +414,15 @@
 def per_device(concentration):
     whole = pl.BlockSpec(memory_space=pltpu.VMEM)
     params = pltpu.CompilerParams(vmem_limit_bytes=12 << 20)
-    outgoing, rate = pl.pallas_call(
+    outgoing, rate, side = pl.pallas_call(
         forward_kernel,
         out_shape=(
             pltpu.VMEM((1280, 128), f32),
-            pltpu.VMEM((8, 128, 128), f32),
+            pltpu.VMEM((4, 128, 128), f32),
+            pltpu.VMEM((4, 32, 128), f32),
         ),
         in_specs=[pl.BlockSpec(memory_space=pltpu.HBM)] * 4,
-        out_specs=(whole, whole),
+        out_specs=(whole, whole, whole),
         scratch_shapes=[
             pltpu.VMEM(concentration.shape, f32),
             pltpu.VMEM(FOURIER.shape, bf16),
@@ -419,10 +436,10 @@
     leaving, bulk = pl.pallas_call(
         middle_kernel,
         out_shape=(pltpu.VMEM((512, 128), f32), pltpu.VMEM((8, 128), f32)),
-        in_specs=[whole] * 6,
+        in_specs=[whole] * 7,
         out_specs=(whole, whole),
         compiler_params=params,
-    )(columns, rate, GATHER, LANES, SPREAD, X_TWIST)
+    )(columns, rate, side, GATHER, LANES, SPREAD, X_TWIST)
     rows_back = exchange(leaving)
     new_field, energy = pl.pallas_call(
         inverse_kernel,

time: 65.2 us -> 65.3 us (level)
  no operation moved by 1% of the time
where the time goes in v9:
time: 65.3 us; the launch traced here: 65.1 us
  blocking collectives  60.1 us (92%)
  Pallas kernels  4.31 us (7%)
  between operations  0.72 us (1%)
    all_to_all x2, blocking collectives, exchange(): lax.all_to_all(message, ALL, split_axis=0, concat_axis=0, tiled=True)  60.1 us
    pallas_call x1, Pallas kernels, per_device(): pl.pallas_call(forward_kernel, out_shape=(pltpu.VMEM((1280, 128), f32), p...  1.75 us
    pallas_call x1, Pallas kernels, per_device(): pl.pallas_call(middle_kernel, out_shape=(pltpu.VMEM((512, 128), f32), plt...  1.47 us

profile of v9, /device:TPU:1, one launch (start us, length us, event | category | flops | bytes accessed | tf_op | source)
XLA Modules:
  0.0 65.1 jit_solution(10980916455038322406)
XLA Ops:
  0.6 1.8 %shard_map.113 = (f32[1280,128]{1,0:T(8,128)S(1)}, f32[4,128,128]{2,1,0:T(8,128)S(1)}, f32[4,32,128]{2,1,0:T(8,128)S(1)}) custom-call(f32[2,16,2048]{2,1,0:T(8,128)} %c_hbm.1, bf16[2,256,256]{2,1,0:T(8,128)(2,1)} %constant.18.clone.fourier_hbm, bf16[2,256,256]{2,1,0:T(8,128)(2,1)} %constant.19.clone.real_hbm, f32[16,128]{1,0:T(8,128)} %constant.20.clone.twist_hbm.twist_ref), custom_call_target="tpu_custom_call" | custom-call | tf_op jit(solution)/shard_map/pallas_call | solution.py:417
  2.4 0.0 copy-start
  2.4 0.0 copy-start.3
  2.4 0.0 copy-start.4
  2.4 0.0 copy-start.5
  2.4 38.6 %all_to_all.10 = f32[256,1,640]{2,1,0:T(1,128)S(1)} all-to-all(f32[256,1,640]{2,1,0:T(1,128)S(1)} %bitcast.7), channel_id=1, replica_groups=mesh['section'=2,'slab_y'=4,'slab_x'=2,'slab_z'=8,'slab_core'=2] {'secti..., dimensions={0} | all-to-all | bytes 1310720 | tf_op jit(solution)/shard_map/all_to_all | solution.py:411
  41.0 0.0 copy-done
  41.0 0.0 copy-done.3
  41.0 0.0 copy-done.4
  41.0 0.0 copy-done.5
  41.0 0.0 copy-start.6
  41.1 1.5 %shard_map.114 = (f32[512,128]{1,0:T(8,128)S(1)}, f32[8,128]{1,0:T(8,128)S(1)}) custom-call(f32[1280,128]{1,0:T(8,128)S(1)} %bitcast.5, f32[4,128,128]{2,1,0:T(8,128)S(1)} %get-tuple-element.10.rate_ref, f32[4,32,128]{2,1,0:T(8,128)S(1)} %get-tuple-element.11.side_ref, bf16[2,256,256]{2,1,0:T(8,128)(2,1)S(1)} %copy-done.3, ...), custom_call_target="tpu_custom_call" | custom-call | tf_op jit(solution)/shard_map/pallas_call | solution.py:436
  42.5 0.0 copy-start.1
  42.5 0.0 copy-start.2
  42.6 21.5 %all_to_all.11 = f32[256,1,256]{2,1,0:T(1,128)S(1)} all-to-all(f32[256,1,256]{2,1,0:T(1,128)S(1)} %bitcast.8), channel_id=1, replica_groups=mesh['section'=2,'slab_y'=4,'slab_x'=2,'slab_z'=8,'slab_core'=2] {'secti..., dimensions={0} | all-to-all | bytes 524288 | tf_op jit(solution)/shard_map/all_to_all | solution.py:411
  64.0 0.0 copy-done.6
  64.0 0.0 copy-done.1
  64.0 0.0 copy-done.2
  64.0 1.1 %shard_map.115 = (f32[2,16,2048]{2,1,0:T(8,128)}, f32[1,1]{1,0:T(1,128)}) custom-call(f32[512,128]{1,0:T(8,128)S(1)} %bitcast.6, f32[8,128]{1,0:T(8,128)S(1)} %get-tuple-element.13.bulk_ref, bf16[2,256,256]{2,1,0:T(8,128)(2,1)S(1)} %copy-done.2, bf16[2,256,256]{2,1,0:T(8,128)(2,1)S(1)} %copy-done.1, f32[16,128]{1,0:T(8,128)S(1)} %copy-done.6), custom_call_target="tpu_custom_call" | custom-call | tf_op jit(solution)/shard_map/pallas_call | solution.py:444
Async XLA Ops:
  2.4 38.6 %copy-start = (bf16[2,2,256,256]{3,2,1,0:T(8,128)(2,1)S(1)}, bf16[2,2,256,256]{3,2,1,0:T(8,128)(2,1)}, u32[]{:S(2)}) copy-start(bf16[2,2,256,256]{3,2,1,0:T(8,128)(2,1)} %constant.22.clone.lanes_ref) | copy-start | bytes 1572868
  2.4 38.6 %copy-start.3 = (bf16[2,256,256]{2,1,0:T(8,128)(2,1)S(1)}, bf16[2,256,256]{2,1,0:T(8,128)(2,1)}, u32[]{:S(2)}) copy-start(bf16[2,256,256]{2,1,0:T(8,128)(2,1)} %constant.21.clone.gather_ref) | copy-start | bytes 786436
  2.4 38.6 %copy-start.4 = (f32[2,128,128]{2,1,0:T(8,128)S(1)}, f32[2,128,128]{2,1,0:T(8,128)}, u32[]{:S(2)}) copy-start(f32[2,128,128]{2,1,0:T(8,128)} %constant.24.clone.twist_ref) | copy-start | bytes 393220
  2.4 38.6 %copy-start.5 = (bf16[2,128,256]{2,1,0:T(8,128)(2,1)S(1)}, bf16[2,128,256]{2,1,0:T(8,128)(2,1)}, u32[]{:S(2)}) copy-start(bf16[2,128,256]{2,1,0:T(8,128)(2,1)} %constant.23.clone.spread_ref) | copy-start | bytes 393220
  41.0 23.0 %copy-start.6 = (f32[16,128]{1,0:T(8,128)S(1)}, f32[16,128]{1,0:T(8,128)}, u32[]{:S(2)}) copy-start(f32[16,128]{1,0:T(8,128)} %constant.20.clone.twist_hbm.twist_ref) | copy-start | bytes 24580
  42.5 21.5 %copy-start.1 = (bf16[2,256,256]{2,1,0:T(8,128)(2,1)S(1)}, bf16[2,256,256]{2,1,0:T(8,128)(2,1)}, u32[]{:S(2)}) copy-start(bf16[2,256,256]{2,1,0:T(8,128)(2,1)} %constant.26.clone.real_ref) | copy-start | bytes 786436
  42.5 21.5 %copy-start.2 = (bf16[2,256,256]{2,1,0:T(8,128)(2,1)S(1)}, bf16[2,256,256]{2,1,0:T(8,128)(2,1)}, u32[]{:S(2)}) copy-start(bf16[2,256,256]{2,1,0:T(8,128)(2,1)} %constant.25.clone.fourier_ref) | copy-start | bytes 786436

commit v10 on v8

--- a/solution.py
+++ b/solution.py
@@ -155,7 +155,7 @@
                 cubic = []
                 for value in block:
                     squared = value * value
-                    bulk = squared * (0.25 * squared - 0.5)
+                    bulk = 0.25 * squared * squared - 0.5 * squared
                     lanes = bulk if lanes is None else lanes + bulk
                     cubic.append(squared * value - value)
                 slots.append(turned_slots(cubic, turns))

time: 65.2 us -> 65.2 us (level)
  no operation moved by 1% of the time
where the time goes in v10:
time: 65.2 us; the launch traced here: 65 us
  blocking collectives  60.1 us (92%)
  Pallas kernels  4.21 us (6%)
  between operations  0.72 us (1%)
    all_to_all x2, blocking collectives, exchange(): lax.all_to_all(message, ALL, split_axis=0, concat_axis=0, tiled=True)  60.1 us
    pallas_call x1, Pallas kernels, per_device(): pl.pallas_call(forward_kernel, out_shape=(pltpu.VMEM((1280, 128), f32), p...  1.75 us
    pallas_call x1, Pallas kernels, per_device(): pl.pallas_call(middle_kernel, out_shape=(pltpu.VMEM((512, 128), f32), plt...  1.38 us

profile of v10, /device:TPU:1, one launch (start us, length us, event | category | flops | bytes accessed | tf_op | source)
XLA Modules:
  0.0 65.0 jit_solution(14181173158556558477)
XLA Ops:
  0.6 1.7 %shard_map.113 = (f32[1280,128]{1,0:T(8,128)S(1)}, f32[8,128,128]{2,1,0:T(8,128)S(1)}) custom-call(f32[2,16,2048]{2,1,0:T(8,128)} %c_hbm.1, bf16[2,256,256]{2,1,0:T(8,128)(2,1)} %constant.18.clone.fourier_hbm, bf16[2,256,256]{2,1,0:T(8,128)(2,1)} %constant.19.clone.real_hbm, f32[16,128]{1,0:T(8,128)} %constant.20.clone.twist_hbm.twist_ref), custom_call_target="tpu_custom_call" | custom-call | tf_op jit(solution)/shard_map/pallas_call | solution.py:401
  2.4 0.0 copy-start
  2.4 0.0 copy-start.3
  2.4 0.0 copy-start.4
  2.4 0.0 copy-start.5
  2.4 38.6 %all_to_all.10 = f32[256,1,640]{2,1,0:T(1,128)S(1)} all-to-all(f32[256,1,640]{2,1,0:T(1,128)S(1)} %bitcast.7), channel_id=1, replica_groups=mesh['section'=2,'slab_y'=4,'slab_x'=2,'slab_z'=8,'slab_core'=2] {'secti..., dimensions={0} | all-to-all | bytes 1310720 | tf_op jit(solution)/shard_map/all_to_all | solution.py:395
  41.0 0.0 copy-done
  41.0 0.0 copy-done.3
  41.0 0.0 copy-done.4
  41.0 0.0 copy-done.5
  41.0 0.0 copy-start.6
  41.0 1.4 %shard_map.114 = (f32[512,128]{1,0:T(8,128)S(1)}, f32[8,128]{1,0:T(8,128)S(1)}) custom-call(f32[1280,128]{1,0:T(8,128)S(1)} %bitcast.5, f32[8,128,128]{2,1,0:T(8,128)S(1)} %get-tuple-element.9.rate_ref, bf16[2,256,256]{2,1,0:T(8,128)(2,1)S(1)} %copy-done.3, bf16[2,2,256,256]{3,2,1,0:T(8,128)(2,1)S(1)} %copy-done, bf16[2,128,256]{2,1,0:T(8,128)(2,1)S(1)} %copy-done.5, ...), custom_call_target="tpu_custom_call" | custom-call | tf_op jit(solution)/shard_map/pallas_call | solution.py:419
  42.4 0.0 copy-start.1
  42.4 0.0 copy-start.2
  42.5 21.5 %all_to_all.11 = f32[256,1,256]{2,1,0:T(1,128)S(1)} all-to-all(f32[256,1,256]{2,1,0:T(1,128)S(1)} %bitcast.8), channel_id=1, replica_groups=mesh['section'=2,'slab_y'=4,'slab_x'=2,'slab_z'=8,'slab_core'=2] {'secti..., dimensions={0} | all-to-all | bytes 524288 | tf_op jit(solution)/shard_map/all_to_all | solution.py:395
  63.9 0.0 copy-done.6
  63.9 0.0 copy-done.1
  63.9 0.0 copy-done.2
  64.0 1.1 %shard_map.115 = (f32[2,16,2048]{2,1,0:T(8,128)}, f32[1,1]{1,0:T(1,128)}) custom-call(f32[512,128]{1,0:T(8,128)S(1)} %bitcast.6, f32[8,128]{1,0:T(8,128)S(1)} %get-tuple-element.11.bulk_ref, bf16[2,256,256]{2,1,0:T(8,128)(2,1)S(1)} %copy-done.2, bf16[2,256,256]{2,1,0:T(8,128)(2,1)S(1)} %copy-done.1, f32[16,128]{1,0:T(8,128)S(1)} %copy-done.6), custom_call_target="tpu_custom_call" | custom-call | tf_op jit(solution)/shard_map/pallas_call | solution.py:427
Async XLA Ops:
  2.4 38.6 %copy-start = (bf16[2,2,256,256]{3,2,1,0:T(8,128)(2,1)S(1)}, bf16[2,2,256,256]{3,2,1,0:T(8,128)(2,1)}, u32[]{:S(2)}) copy-start(bf16[2,2,256,256]{3,2,1,0:T(8,128)(2,1)} %constant.22.clone.lanes_ref) | copy-start | bytes 1572868
  2.4 38.6 %copy-start.3 = (bf16[2,256,256]{2,1,0:T(8,128)(2,1)S(1)}, bf16[2,256,256]{2,1,0:T(8,128)(2,1)}, u32[]{:S(2)}) copy-start(bf16[2,256,256]{2,1,0:T(8,128)(2,1)} %constant.21.clone.gather_ref) | copy-start | bytes 786436
  2.4 38.6 %copy-start.4 = (f32[2,128,128]{2,1,0:T(8,128)S(1)}, f32[2,128,128]{2,1,0:T(8,128)}, u32[]{:S(2)}) copy-start(f32[2,128,128]{2,1,0:T(8,128)} %constant.24.clone.twist_ref) | copy-start | bytes 393220
  2.4 38.6 %copy-start.5 = (bf16[2,128,256]{2,1,0:T(8,128)(2,1)S(1)}, bf16[2,128,256]{2,1,0:T(8,128)(2,1)}, u32[]{:S(2)}) copy-start(bf16[2,128,256]{2,1,0:T(8,128)(2,1)} %constant.23.clone.spread_ref) | copy-start | bytes 393220
  41.0 22.9 %copy-start.6 = (f32[16,128]{1,0:T(8,128)S(1)}, f32[16,128]{1,0:T(8,128)}, u32[]{:S(2)}) copy-start(f32[16,128]{1,0:T(8,128)} %constant.20.clone.twist_hbm.twist_ref) | copy-start | bytes 24580
  42.4 21.5 %copy-start.1 = (bf16[2,256,256]{2,1,0:T(8,128)(2,1)S(1)}, bf16[2,256,256]{2,1,0:T(8,128)(2,1)}, u32[]{:S(2)}) copy-start(bf16[2,256,256]{2,1,0:T(8,128)(2,1)} %constant.26.clone.real_ref) | copy-start | bytes 786436
  42.4 21.5 %copy-start.2 = (bf16[2,256,256]{2,1,0:T(8,128)(2,1)S(1)}, bf16[2,256,256]{2,1,0:T(8,128)(2,1)}, u32[]{:S(2)}) copy-start(bf16[2,256,256]{2,1,0:T(8,128)(2,1)} %constant.25.clone.fourier_ref) | copy-start | bytes 786436

commit v11 on v10

--- a/solution.py
+++ b/solution.py
@@ -155,7 +155,8 @@
                 cubic = []
                 for value in block:
                     squared = value * value
-                    bulk = 0.25 * squared * squared - 0.5 * squared
+                    half = 0.5 * squared
+                    bulk = half * half - half
                     lanes = bulk if lanes is None else lanes + bulk
                     cubic.append(squared * value - value)
                 slots.append(turned_slots(cubic, turns))

time: 65.2 us -> 65.2 us (level)
  no operation moved by 1% of the time
where the time goes in v11:
time: 65.2 us; the launch traced here: 65 us
  blocking collectives  60.1 us (92%)
  Pallas kernels  4.22 us (6%)
  between operations  0.72 us (1%)
    all_to_all x2, blocking collectives, exchange(): lax.all_to_all(message, ALL, split_axis=0, concat_axis=0, tiled=True)  60.1 us
    pallas_call x1, Pallas kernels, per_device(): pl.pallas_call(forward_kernel, out_shape=(pltpu.VMEM((1280, 128), f32), p...  1.75 us
    pallas_call x1, Pallas kernels, per_device(): pl.pallas_call(middle_kernel, out_shape=(pltpu.VMEM((512, 128), f32), plt...  1.38 us

profile of v11, /device:TPU:1, one launch (start us, length us, event | category | flops | bytes accessed | tf_op | source)
XLA Modules:
  0.0 65.0 jit_solution(5440510754206984969)
XLA Ops:
  0.6 1.8 %shard_map.113 = (f32[1280,128]{1,0:T(8,128)S(1)}, f32[8,128,128]{2,1,0:T(8,128)S(1)}) custom-call(f32[2,16,2048]{2,1,0:T(8,128)} %c_hbm.1, bf16[2,256,256]{2,1,0:T(8,128)(2,1)} %constant.18.clone.fourier_hbm, bf16[2,256,256]{2,1,0:T(8,128)(2,1)} %constant.19.clone.real_hbm, f32[16,128]{1,0:T(8,128)} %constant.20.clone.twist_hbm.twist_ref), custom_call_target="tpu_custom_call" | custom-call | tf_op jit(solution)/shard_map/pallas_call | solution.py:402
  2.4 0.0 copy-start
  2.4 0.0 copy-start.3
  2.4 0.0 copy-start.4
  2.4 0.0 copy-start.5
  2.4 38.6 %all_to_all.10 = f32[256,1,640]{2,1,0:T(1,128)S(1)} all-to-all(f32[256,1,640]{2,1,0:T(1,128)S(1)} %bitcast.7), channel_id=1, replica_groups=mesh['section'=2,'slab_y'=4,'slab_x'=2,'slab_z'=8,'slab_core'=2] {'secti..., dimensions={0} | all-to-all | bytes 1310720 | tf_op jit(solution)/shard_map/all_to_all | solution.py:396
  41.0 0.0 copy-done
  41.0 0.0 copy-done.3
  41.0 0.0 copy-done.4
  41.0 0.0 copy-done.5
  41.0 0.0 copy-start.6
  41.1 1.4 %shard_map.114 = (f32[512,128]{1,0:T(8,128)S(1)}, f32[8,128]{1,0:T(8,128)S(1)}) custom-call(f32[1280,128]{1,0:T(8,128)S(1)} %bitcast.5, f32[8,128,128]{2,1,0:T(8,128)S(1)} %get-tuple-element.9.rate_ref, bf16[2,256,256]{2,1,0:T(8,128)(2,1)S(1)} %copy-done.3, bf16[2,2,256,256]{3,2,1,0:T(8,128)(2,1)S(1)} %copy-done, bf16[2,128,256]{2,1,0:T(8,128)(2,1)S(1)} %copy-done.5, ...), custom_call_target="tpu_custom_call" | custom-call | tf_op jit(solution)/shard_map/pallas_call | solution.py:420
  42.4 0.0 copy-start.1
  42.5 0.0 copy-start.2
  42.5 21.5 %all_to_all.11 = f32[256,1,256]{2,1,0:T(1,128)S(1)} all-to-all(f32[256,1,256]{2,1,0:T(1,128)S(1)} %bitcast.8), channel_id=1, replica_groups=mesh['section'=2,'slab_y'=4,'slab_x'=2,'slab_z'=8,'slab_core'=2] {'secti..., dimensions={0} | all-to-all | bytes 524288 | tf_op jit(solution)/shard_map/all_to_all | solution.py:396
  63.9 0.0 copy-done.6
  64.0 0.0 copy-done.1
  64.0 0.0 copy-done.2
  64.0 1.1 %shard_map.115 = (f32[2,16,2048]{2,1,0:T(8,128)}, f32[1,1]{1,0:T(1,128)}) custom-call(f32[512,128]{1,0:T(8,128)S(1)} %bitcast.6, f32[8,128]{1,0:T(8,128)S(1)} %get-tuple-element.11.bulk_ref, bf16[2,256,256]{2,1,0:T(8,128)(2,1)S(1)} %copy-done.2, bf16[2,256,256]{2,1,0:T(8,128)(2,1)S(1)} %copy-done.1, f32[16,128]{1,0:T(8,128)S(1)} %copy-done.6), custom_call_target="tpu_custom_call" | custom-call | tf_op jit(solution)/shard_map/pallas_call | solution.py:428
Async XLA Ops:
  2.4 38.6 %copy-start = (bf16[2,2,256,256]{3,2,1,0:T(8,128)(2,1)S(1)}, bf16[2,2,256,256]{3,2,1,0:T(8,128)(2,1)}, u32[]{:S(2)}) copy-start(bf16[2,2,256,256]{3,2,1,0:T(8,128)(2,1)} %constant.22.clone.lanes_ref) | copy-start | bytes 1572868
  2.4 38.6 %copy-start.3 = (bf16[2,256,256]{2,1,0:T(8,128)(2,1)S(1)}, bf16[2,256,256]{2,1,0:T(8,128)(2,1)}, u32[]{:S(2)}) copy-start(bf16[2,256,256]{2,1,0:T(8,128)(2,1)} %constant.21.clone.gather_ref) | copy-start | bytes 786436
  2.4 38.6 %copy-start.4 = (f32[2,128,128]{2,1,0:T(8,128)S(1)}, f32[2,128,128]{2,1,0:T(8,128)}, u32[]{:S(2)}) copy-start(f32[2,128,128]{2,1,0:T(8,128)} %constant.24.clone.twist_ref) | copy-start | bytes 393220
  2.4 38.6 %copy-start.5 = (bf16[2,128,256]{2,1,0:T(8,128)(2,1)S(1)}, bf16[2,128,256]{2,1,0:T(8,128)(2,1)}, u32[]{:S(2)}) copy-start(bf16[2,128,256]{2,1,0:T(8,128)(2,1)} %constant.23.clone.spread_ref) | copy-start | bytes 393220
  41.0 22.9 %copy-start.6 = (f32[16,128]{1,0:T(8,128)S(1)}, f32[16,128]{1,0:T(8,128)}, u32[]{:S(2)}) copy-start(f32[16,128]{1,0:T(8,128)} %constant.20.clone.twist_hbm.twist_ref) | copy-start | bytes 24580
  42.4 21.5 %copy-start.1 = (bf16[2,256,256]{2,1,0:T(8,128)(2,1)S(1)}, bf16[2,256,256]{2,1,0:T(8,128)(2,1)}, u32[]{:S(2)}) copy-start(bf16[2,256,256]{2,1,0:T(8,128)(2,1)} %constant.26.clone.real_ref) | copy-start | bytes 786436
  42.5 21.5 %copy-start.2 = (bf16[2,256,256]{2,1,0:T(8,128)(2,1)S(1)}, bf16[2,256,256]{2,1,0:T(8,128)(2,1)}, u32[]{:S(2)}) copy-start(bf16[2,256,256]{2,1,0:T(8,128)(2,1)} %constant.25.clone.fourier_ref) | copy-start | bytes 786436

commit v12 on v8

--- a/solution.py
+++ b/solution.py
@@ -11,7 +11,7 @@
 from jax.sharding import PartitionSpec as P
 
 SLAB = ("slab_y", "slab_x", "slab_z", "slab_core")
-ALL = ("section", "slab_z", "slab_y", "slab_x", "slab_core")
+ALL = ("slab_z", "slab_x", "slab_y", "slab_core", "section")
 NX = 2048
 NY = 2048
 NZ = 4
@@ -36,7 +36,7 @@
 
 
 def slab_order():
-    return np.arange(128).reshape(4, 2, 8, 2).transpose(2, 0, 1, 3).reshape(128)
+    return np.arange(128).reshape(4, 2, 8, 2).transpose(2, 1, 0, 3).reshape(128)
 
 
 def real_table():
@@ -298,8 +298,8 @@
 def lane_position():
     return (
         16 * lax.axis_index("slab_z")
-        + 4 * lax.axis_index("slab_y")
-        + 2 * lax.axis_index("slab_x")
+        + 8 * lax.axis_index("slab_x")
+        + 2 * lax.axis_index("slab_y")
         + lax.axis_index("slab_core")
     )
 
@@ -330,7 +330,7 @@
         copy.start()
 
     def put(h, part, f, value):
-        out_ref[pl.ds(640 * h + 2 * part + f, 128, stride=5), :] = value
+        out_ref[pl.ds(5 * h + 2 * part + f, 128, stride=10), :] = value
 
     def put_rate(sigma, side, kind, value):
         rate_ref[4 * sigma + 2 * side + kind] = value
@@ -355,10 +355,10 @@
     in_ref, rate_ref, gather_ref, lanes_ref, spread_ref, twist_ref, out_ref, bulk_ref
 ):
     def get(s, part, f):
-        return in_ref[pl.ds(640 * s + 2 * part + f, 128, stride=5), :]
+        return in_ref[pl.ds(5 * s + 2 * part + f, 128, stride=10), :]
 
     def put(s, part, value):
-        out_ref[pl.ds(256 * s + part, 128, stride=2), :] = value
+        out_ref[pl.ds(2 * s + part, 128, stride=4), :] = value
 
     middle(
         get,
@@ -377,7 +377,7 @@
 
 def inverse_kernel(in_ref, bulk_ref, fourier_ref, real_ref, twist_ref, out_ref, energy_ref):
     def get(h, part):
-        return in_ref[pl.ds(256 * h + part, 128, stride=2), :]
+        return in_ref[pl.ds(2 * h + part, 128, stride=4), :]
 
     def put(a, value):
         out_ref[0, :, 128 * a : 128 * a + 128] = value[:16]

time: 65.2 us -> 64.7 us (level)
  no operation moved by 1% of the time
where the time goes in v12:
time: 64.7 us; the launch traced here: 64.5 us
  blocking collectives  59.6 us (92%)
  Pallas kernels  4.22 us (7%)
  between operations  0.72 us (1%)
    all_to_all x2, blocking collectives, exchange(): lax.all_to_all(message, ALL, split_axis=0, concat_axis=0, tiled=True)  59.6 us
    pallas_call x1, Pallas kernels, per_device(): pl.pallas_call(forward_kernel, out_shape=(pltpu.VMEM((1280, 128), f32), p...  1.75 us
    pallas_call x1, Pallas kernels, per_device(): pl.pallas_call(middle_kernel, out_shape=(pltpu.VMEM((512, 128), f32), plt...  1.38 us

profile of v12, /device:TPU:1, one launch (start us, length us, event | category | flops | bytes accessed | tf_op | source)
XLA Modules:
  0.0 64.5 jit_solution(13865756800750615428)
XLA Ops:
  0.6 1.8 %shard_map.113 = (f32[1280,128]{1,0:T(8,128)S(1)}, f32[8,128,128]{2,1,0:T(8,128)S(1)}) custom-call(f32[2,16,2048]{2,1,0:T(8,128)} %c_hbm.1, bf16[2,256,256]{2,1,0:T(8,128)(2,1)} %constant.18.clone.fourier_hbm, bf16[2,256,256]{2,1,0:T(8,128)(2,1)} %constant.19.clone.real_hbm, f32[16,128]{1,0:T(8,128)} %constant.20.clone.twist_hbm.twist_ref), custom_call_target="tpu_custom_call" | custom-call | tf_op jit(solution)/shard_map/pallas_call | solution.py:401
  2.4 0.0 copy-start
  2.4 0.0 copy-start.3
  2.4 0.0 copy-start.4
  2.4 0.0 copy-start.5
  2.4 38.2 %all_to_all.10 = f32[256,1,640]{2,1,0:T(1,128)S(1)} all-to-all(f32[256,1,640]{2,1,0:T(1,128)S(1)} %bitcast.7), channel_id=1, replica_groups=mesh['section'=2,'slab_y'=4,'slab_x'=2,'slab_z'=8,'slab_core'=2] {'slab_..., dimensions={0} | all-to-all | bytes 1310720 | tf_op jit(solution)/shard_map/all_to_all | solution.py:395
  40.6 0.0 copy-done
  40.6 0.0 copy-done.3
  40.6 0.0 copy-done.4
  40.6 0.0 copy-done.5
  40.6 0.0 copy-start.6
  40.7 1.4 %shard_map.114 = (f32[512,128]{1,0:T(8,128)S(1)}, f32[8,128]{1,0:T(8,128)S(1)}) custom-call(f32[1280,128]{1,0:T(8,128)S(1)} %bitcast.5, f32[8,128,128]{2,1,0:T(8,128)S(1)} %get-tuple-element.9.rate_ref, bf16[2,256,256]{2,1,0:T(8,128)(2,1)S(1)} %copy-done.3, bf16[2,2,256,256]{3,2,1,0:T(8,128)(2,1)S(1)} %copy-done, bf16[2,128,256]{2,1,0:T(8,128)(2,1)S(1)} %copy-done.5, ...), custom_call_target="tpu_custom_call" | custom-call | tf_op jit(solution)/shard_map/pallas_call | solution.py:419
  42.0 0.0 copy-start.1
  42.1 0.0 copy-start.2
  42.1 21.4 %all_to_all.11 = f32[256,1,256]{2,1,0:T(1,128)S(1)} all-to-all(f32[256,1,256]{2,1,0:T(1,128)S(1)} %bitcast.8), channel_id=1, replica_groups=mesh['section'=2,'slab_y'=4,'slab_x'=2,'slab_z'=8,'slab_core'=2] {'slab_..., dimensions={0} | all-to-all | bytes 524288 | tf_op jit(solution)/shard_map/all_to_all | solution.py:395
  63.4 0.0 copy-done.6
  63.4 0.0 copy-done.1
  63.5 0.0 copy-done.2
  63.5 1.1 %shard_map.115 = (f32[2,16,2048]{2,1,0:T(8,128)}, f32[1,1]{1,0:T(1,128)}) custom-call(f32[512,128]{1,0:T(8,128)S(1)} %bitcast.6, f32[8,128]{1,0:T(8,128)S(1)} %get-tuple-element.11.bulk_ref, bf16[2,256,256]{2,1,0:T(8,128)(2,1)S(1)} %copy-done.2, bf16[2,256,256]{2,1,0:T(8,128)(2,1)S(1)} %copy-done.1, f32[16,128]{1,0:T(8,128)S(1)} %copy-done.6), custom_call_target="tpu_custom_call" | custom-call | tf_op jit(solution)/shard_map/pallas_call | solution.py:427
Async XLA Ops:
  2.4 38.2 %copy-start = (bf16[2,2,256,256]{3,2,1,0:T(8,128)(2,1)S(1)}, bf16[2,2,256,256]{3,2,1,0:T(8,128)(2,1)}, u32[]{:S(2)}) copy-start(bf16[2,2,256,256]{3,2,1,0:T(8,128)(2,1)} %constant.22.clone.lanes_ref) | copy-start | bytes 1572868
  2.4 38.2 %copy-start.3 = (bf16[2,256,256]{2,1,0:T(8,128)(2,1)S(1)}, bf16[2,256,256]{2,1,0:T(8,128)(2,1)}, u32[]{:S(2)}) copy-start(bf16[2,256,256]{2,1,0:T(8,128)(2,1)} %constant.21.clone.gather_ref) | copy-start | bytes 786436
  2.4 38.2 %copy-start.4 = (f32[2,128,128]{2,1,0:T(8,128)S(1)}, f32[2,128,128]{2,1,0:T(8,128)}, u32[]{:S(2)}) copy-start(f32[2,128,128]{2,1,0:T(8,128)} %constant.24.clone.twist_ref) | copy-start | bytes 393220
  2.4 38.2 %copy-start.5 = (bf16[2,128,256]{2,1,0:T(8,128)(2,1)S(1)}, bf16[2,128,256]{2,1,0:T(8,128)(2,1)}, u32[]{:S(2)}) copy-start(bf16[2,128,256]{2,1,0:T(8,128)(2,1)} %constant.23.clone.spread_ref) | copy-start | bytes 393220
  40.6 22.8 %copy-start.6 = (f32[16,128]{1,0:T(8,128)S(1)}, f32[16,128]{1,0:T(8,128)}, u32[]{:S(2)}) copy-start(f32[16,128]{1,0:T(8,128)} %constant.20.clone.twist_hbm.twist_ref) | copy-start | bytes 24580
  42.0 21.4 %copy-start.1 = (bf16[2,256,256]{2,1,0:T(8,128)(2,1)S(1)}, bf16[2,256,256]{2,1,0:T(8,128)(2,1)}, u32[]{:S(2)}) copy-start(bf16[2,256,256]{2,1,0:T(8,128)(2,1)} %constant.26.clone.real_ref) | copy-start | bytes 786436
  42.1 21.4 %copy-start.2 = (bf16[2,256,256]{2,1,0:T(8,128)(2,1)S(1)}, bf16[2,256,256]{2,1,0:T(8,128)(2,1)}, u32[]{:S(2)}) copy-start(bf16[2,256,256]{2,1,0:T(8,128)(2,1)} %constant.25.clone.fourier_ref) | copy-start | bytes 786436

commit v13 on v12

--- a/solution.py
+++ b/solution.py
@@ -68,7 +68,7 @@
 FOURIER = fourier_table()
 ORDER = slab_order()
 GATHER = FOURIER[:, :, np.concatenate([ORDER, 128 + ORDER])]
-SPREAD = FOURIER[:, ORDER, :]
+SPREAD = np.concatenate([FOURIER[:, ORDER, :128], -FOURIER[:, ORDER, 128:]], 2)
 REAL = real_table()
 LANES = np.stack([lane_table(0), lane_table(1)])
 FOURIER_T = FOURIER.transpose(0, 2, 1)
@@ -246,7 +246,7 @@
             both.append((re * cos - im * sin, im * cos + re * sin))
         (m_re, m_im), (s_re, s_im) = both
         upper = jnp.concatenate([m_re, jnp.where(packed, s_re, m_im)], 1)
-        lower = jnp.concatenate([-m_im, jnp.where(packed, -s_im, m_re)], 1)
+        lower = jnp.concatenate([m_im, jnp.where(packed, s_im, -m_re)], 1)
         out = product(spread_table, split(jnp.concatenate([upper, lower], 0)), NN)
         put(s, 0, out[:, :128])
         put(s, 1, out[:, 128:])

time: 64.7 us -> 64.7 us (level)
  no operation moved by 1% of the time
where the time goes in v13:
time: 64.7 us; the launch traced here: 64.5 us
  blocking collectives  59.6 us (92%)
  Pallas kernels  4.2 us (6%)
  between operations  0.72 us (1%)
    all_to_all x2, blocking collectives, exchange(): lax.all_to_all(message, ALL, split_axis=0, concat_axis=0, tiled=True)  59.6 us
    pallas_call x1, Pallas kernels, per_device(): pl.pallas_call(forward_kernel, out_shape=(pltpu.VMEM((1280, 128), f32), p...  1.75 us
    pallas_call x1, Pallas kernels, per_device(): pl.pallas_call(middle_kernel, out_shape=(pltpu.VMEM((512, 128), f32), plt...  1.37 us

profile of v13, /device:TPU:1, one launch (start us, length us, event | category | flops | bytes accessed | tf_op | source)
XLA Modules:
  0.0 64.5 jit_solution(9938289552406486049)
XLA Ops:
  0.6 1.8 %shard_map.113 = (f32[1280,128]{1,0:T(8,128)S(1)}, f32[8,128,128]{2,1,0:T(8,128)S(1)}) custom-call(f32[2,16,2048]{2,1,0:T(8,128)} %c_hbm.1, bf16[2,256,256]{2,1,0:T(8,128)(2,1)} %constant.18.clone.fourier_hbm, bf16[2,256,256]{2,1,0:T(8,128)(2,1)} %constant.19.clone.real_hbm, f32[16,128]{1,0:T(8,128)} %constant.20.clone.twist_hbm.twist_ref), custom_call_target="tpu_custom_call" | custom-call | tf_op jit(solution)/shard_map/pallas_call | solution.py:401
  2.4 0.0 copy-start
  2.4 0.0 copy-start.3
  2.4 0.0 copy-start.4
  2.4 0.0 copy-start.5
  2.4 38.2 %all_to_all.10 = f32[256,1,640]{2,1,0:T(1,128)S(1)} all-to-all(f32[256,1,640]{2,1,0:T(1,128)S(1)} %bitcast.7), channel_id=1, replica_groups=mesh['section'=2,'slab_y'=4,'slab_x'=2,'slab_z'=8,'slab_core'=2] {'slab_..., dimensions={0} | all-to-all | bytes 1310720 | tf_op jit(solution)/shard_map/all_to_all | solution.py:395
  40.6 0.0 copy-done
  40.6 0.0 copy-done.3
  40.6 0.0 copy-done.4
  40.6 0.0 copy-done.5
  40.6 0.0 copy-start.6
  40.7 1.4 %shard_map.114 = (f32[512,128]{1,0:T(8,128)S(1)}, f32[8,128]{1,0:T(8,128)S(1)}) custom-call(f32[1280,128]{1,0:T(8,128)S(1)} %bitcast.5, f32[8,128,128]{2,1,0:T(8,128)S(1)} %get-tuple-element.9.rate_ref, bf16[2,256,256]{2,1,0:T(8,128)(2,1)S(1)} %copy-done.3, bf16[2,2,256,256]{3,2,1,0:T(8,128)(2,1)S(1)} %copy-done, bf16[2,128,256]{2,1,0:T(8,128)(2,1)S(1)} %copy-done.5, ...), custom_call_target="tpu_custom_call" | custom-call | tf_op jit(solution)/shard_map/pallas_call | solution.py:419
  42.0 0.0 copy-start.1
  42.0 0.0 copy-start.2
  42.1 21.4 %all_to_all.11 = f32[256,1,256]{2,1,0:T(1,128)S(1)} all-to-all(f32[256,1,256]{2,1,0:T(1,128)S(1)} %bitcast.8), channel_id=1, replica_groups=mesh['section'=2,'slab_y'=4,'slab_x'=2,'slab_z'=8,'slab_core'=2] {'slab_..., dimensions={0} | all-to-all | bytes 524288 | tf_op jit(solution)/shard_map/all_to_all | solution.py:395
  63.4 0.0 copy-done.6
  63.4 0.0 copy-done.1
  63.4 0.0 copy-done.2
  63.4 1.1 %shard_map.115 = (f32[2,16,2048]{2,1,0:T(8,128)}, f32[1,1]{1,0:T(1,128)}) custom-call(f32[512,128]{1,0:T(8,128)S(1)} %bitcast.6, f32[8,128]{1,0:T(8,128)S(1)} %get-tuple-element.11.bulk_ref, bf16[2,256,256]{2,1,0:T(8,128)(2,1)S(1)} %copy-done.2, bf16[2,256,256]{2,1,0:T(8,128)(2,1)S(1)} %copy-done.1, f32[16,128]{1,0:T(8,128)S(1)} %copy-done.6), custom_call_target="tpu_custom_call" | custom-call | tf_op jit(solution)/shard_map/pallas_call | solution.py:427
Async XLA Ops:
  2.4 38.2 %copy-start = (bf16[2,2,256,256]{3,2,1,0:T(8,128)(2,1)S(1)}, bf16[2,2,256,256]{3,2,1,0:T(8,128)(2,1)}, u32[]{:S(2)}) copy-start(bf16[2,2,256,256]{3,2,1,0:T(8,128)(2,1)} %constant.22.clone.lanes_ref) | copy-start | bytes 1572868
  2.4 38.2 %copy-start.3 = (bf16[2,256,256]{2,1,0:T(8,128)(2,1)S(1)}, bf16[2,256,256]{2,1,0:T(8,128)(2,1)}, u32[]{:S(2)}) copy-start(bf16[2,256,256]{2,1,0:T(8,128)(2,1)} %constant.21.clone.gather_ref) | copy-start | bytes 786436
  2.4 38.2 %copy-start.4 = (f32[2,128,128]{2,1,0:T(8,128)S(1)}, f32[2,128,128]{2,1,0:T(8,128)}, u32[]{:S(2)}) copy-start(f32[2,128,128]{2,1,0:T(8,128)} %constant.24.clone.twist_ref) | copy-start | bytes 393220
  2.4 38.2 %copy-start.5 = (bf16[2,128,256]{2,1,0:T(8,128)(2,1)S(1)}, bf16[2,128,256]{2,1,0:T(8,128)(2,1)}, u32[]{:S(2)}) copy-start(bf16[2,128,256]{2,1,0:T(8,128)(2,1)} %constant.23.clone.spread_ref) | copy-start | bytes 393220
  40.6 22.8 %copy-start.6 = (f32[16,128]{1,0:T(8,128)S(1)}, f32[16,128]{1,0:T(8,128)}, u32[]{:S(2)}) copy-start(f32[16,128]{1,0:T(8,128)} %constant.20.clone.twist_hbm.twist_ref) | copy-start | bytes 24580
  42.0 21.4 %copy-start.1 = (bf16[2,256,256]{2,1,0:T(8,128)(2,1)S(1)}, bf16[2,256,256]{2,1,0:T(8,128)(2,1)}, u32[]{:S(2)}) copy-start(bf16[2,256,256]{2,1,0:T(8,128)(2,1)} %constant.26.clone.real_ref) | copy-start | bytes 786436
  42.0 21.4 %copy-start.2 = (bf16[2,256,256]{2,1,0:T(8,128)(2,1)S(1)}, bf16[2,256,256]{2,1,0:T(8,128)(2,1)}, u32[]{:S(2)}) copy-start(bf16[2,256,256]{2,1,0:T(8,128)(2,1)} %constant.25.clone.fourier_ref) | copy-start | bytes 786436

commit v14 on v12

--- a/solution.py
+++ b/solution.py
@@ -11,7 +11,7 @@
 from jax.sharding import PartitionSpec as P
 
 SLAB = ("slab_y", "slab_x", "slab_z", "slab_core")
-ALL = ("slab_z", "slab_x", "slab_y", "slab_core", "section")
+ALL = ("slab_x", "slab_z", "slab_y", "slab_core", "section")
 NX = 2048
 NY = 2048
 NZ = 4
@@ -36,7 +36,7 @@
 
 
 def slab_order():
-    return np.arange(128).reshape(4, 2, 8, 2).transpose(2, 1, 0, 3).reshape(128)
+    return np.arange(128).reshape(4, 2, 8, 2).transpose(1, 2, 0, 3).reshape(128)
 
 
 def real_table():
@@ -297,8 +297,8 @@
 
 def lane_position():
     return (
-        16 * lax.axis_index("slab_z")
-        + 8 * lax.axis_index("slab_x")
+        8 * lax.axis_index("slab_z")
+        + 64 * lax.axis_index("slab_x")
         + 2 * lax.axis_index("slab_y")
         + lax.axis_index("slab_core")
     )

time: 64.7 us -> 64.9 us (level)
  no operation moved by 1% of the time
where the time goes in v14:
time: 64.9 us; the launch traced here: 64.7 us
  blocking collectives  59.8 us (92%)
  Pallas kernels  4.21 us (6%)
  between operations  0.72 us (1%)
    all_to_all x2, blocking collectives, exchange(): lax.all_to_all(message, ALL, split_axis=0, concat_axis=0, tiled=True)  59.8 us
    pallas_call x1, Pallas kernels, per_device(): pl.pallas_call(forward_kernel, out_shape=(pltpu.VMEM((1280, 128), f32), p...  1.75 us
    pallas_call x1, Pallas kernels, per_device(): pl.pallas_call(middle_kernel, out_shape=(pltpu.VMEM((512, 128), f32), plt...  1.37 us

profile of v14, /device:TPU:1, one launch (start us, length us, event | category | flops | bytes accessed | tf_op | source)
XLA Modules:
  0.0 64.7 jit_solution(2528657626872600981)
XLA Ops:
  0.6 1.8 %shard_map.113 = (f32[1280,128]{1,0:T(8,128)S(1)}, f32[8,128,128]{2,1,0:T(8,128)S(1)}) custom-call(f32[2,16,2048]{2,1,0:T(8,128)} %c_hbm.1, bf16[2,256,256]{2,1,0:T(8,128)(2,1)} %constant.18.clone.fourier_hbm, bf16[2,256,256]{2,1,0:T(8,128)(2,1)} %constant.19.clone.real_hbm, f32[16,128]{1,0:T(8,128)} %constant.20.clone.twist_hbm.twist_ref), custom_call_target="tpu_custom_call" | custom-call | tf_op jit(solution)/shard_map/pallas_call | solution.py:401
  2.4 0.0 copy-start
  2.4 0.0 copy-start.3
  2.4 0.0 copy-start.4
  2.4 0.0 copy-start.5
  2.4 38.3 %all_to_all.10 = f32[256,1,640]{2,1,0:T(1,128)S(1)} all-to-all(f32[256,1,640]{2,1,0:T(1,128)S(1)} %bitcast.7), channel_id=1, replica_groups=mesh['section'=2,'slab_y'=4,'slab_x'=2,'slab_z'=8,'slab_core'=2] {'slab_..., dimensions={0} | all-to-all | bytes 1310720 | tf_op jit(solution)/shard_map/all_to_all | solution.py:395
  40.7 0.0 copy-done
  40.7 0.0 copy-done.3
  40.7 0.0 copy-done.4
  40.7 0.0 copy-done.5
  40.7 0.0 copy-start.6
  40.8 1.4 %shard_map.114 = (f32[512,128]{1,0:T(8,128)S(1)}, f32[8,128]{1,0:T(8,128)S(1)}) custom-call(f32[1280,128]{1,0:T(8,128)S(1)} %bitcast.5, f32[8,128,128]{2,1,0:T(8,128)S(1)} %get-tuple-element.9.rate_ref, bf16[2,256,256]{2,1,0:T(8,128)(2,1)S(1)} %copy-done.3, bf16[2,2,256,256]{3,2,1,0:T(8,128)(2,1)S(1)} %copy-done, bf16[2,128,256]{2,1,0:T(8,128)(2,1)S(1)} %copy-done.5, ...), custom_call_target="tpu_custom_call" | custom-call | tf_op jit(solution)/shard_map/pallas_call | solution.py:419
  42.1 0.0 copy-start.1
  42.1 0.0 copy-start.2
  42.2 21.5 %all_to_all.11 = f32[256,1,256]{2,1,0:T(1,128)S(1)} all-to-all(f32[256,1,256]{2,1,0:T(1,128)S(1)} %bitcast.8), channel_id=1, replica_groups=mesh['section'=2,'slab_y'=4,'slab_x'=2,'slab_z'=8,'slab_core'=2] {'slab_..., dimensions={0} | all-to-all | bytes 524288 | tf_op jit(solution)/shard_map/all_to_all | solution.py:395
  63.6 0.0 copy-done.6
  63.6 0.0 copy-done.1
  63.6 0.0 copy-done.2
  63.7 1.1 %shard_map.115 = (f32[2,16,2048]{2,1,0:T(8,128)}, f32[1,1]{1,0:T(1,128)}) custom-call(f32[512,128]{1,0:T(8,128)S(1)} %bitcast.6, f32[8,128]{1,0:T(8,128)S(1)} %get-tuple-element.11.bulk_ref, bf16[2,256,256]{2,1,0:T(8,128)(2,1)S(1)} %copy-done.2, bf16[2,256,256]{2,1,0:T(8,128)(2,1)S(1)} %copy-done.1, f32[16,128]{1,0:T(8,128)S(1)} %copy-done.6), custom_call_target="tpu_custom_call" | custom-call | tf_op jit(solution)/shard_map/pallas_call | solution.py:427
Async XLA Ops:
  2.4 38.3 %copy-start = (bf16[2,2,256,256]{3,2,1,0:T(8,128)(2,1)S(1)}, bf16[2,2,256,256]{3,2,1,0:T(8,128)(2,1)}, u32[]{:S(2)}) copy-start(bf16[2,2,256,256]{3,2,1,0:T(8,128)(2,1)} %constant.22.clone.lanes_ref) | copy-start | bytes 1572868
  2.4 38.3 %copy-start.3 = (bf16[2,256,256]{2,1,0:T(8,128)(2,1)S(1)}, bf16[2,256,256]{2,1,0:T(8,128)(2,1)}, u32[]{:S(2)}) copy-start(bf16[2,256,256]{2,1,0:T(8,128)(2,1)} %constant.21.clone.gather_ref) | copy-start | bytes 786436
  2.4 38.3 %copy-start.4 = (f32[2,128,128]{2,1,0:T(8,128)S(1)}, f32[2,128,128]{2,1,0:T(8,128)}, u32[]{:S(2)}) copy-start(f32[2,128,128]{2,1,0:T(8,128)} %constant.24.clone.twist_ref) | copy-start | bytes 393220
  2.4 38.3 %copy-start.5 = (bf16[2,128,256]{2,1,0:T(8,128)(2,1)S(1)}, bf16[2,128,256]{2,1,0:T(8,128)(2,1)}, u32[]{:S(2)}) copy-start(bf16[2,128,256]{2,1,0:T(8,128)(2,1)} %constant.23.clone.spread_ref) | copy-start | bytes 393220
  40.7 22.9 %copy-start.6 = (f32[16,128]{1,0:T(8,128)S(1)}, f32[16,128]{1,0:T(8,128)}, u32[]{:S(2)}) copy-start(f32[16,128]{1,0:T(8,128)} %constant.20.clone.twist_hbm.twist_ref) | copy-start | bytes 24580
  42.1 21.5 %copy-start.1 = (bf16[2,256,256]{2,1,0:T(8,128)(2,1)S(1)}, bf16[2,256,256]{2,1,0:T(8,128)(2,1)}, u32[]{:S(2)}) copy-start(bf16[2,256,256]{2,1,0:T(8,128)(2,1)} %constant.26.clone.real_ref) | copy-start | bytes 786436
  42.1 21.5 %copy-start.2 = (bf16[2,256,256]{2,1,0:T(8,128)(2,1)S(1)}, bf16[2,256,256]{2,1,0:T(8,128)(2,1)}, u32[]{:S(2)}) copy-start(bf16[2,256,256]{2,1,0:T(8,128)(2,1)} %constant.25.clone.fourier_ref) | copy-start | bytes 786436
